TPU v7x, 8 devices: a whole 2x2x1 slice. The times are simulated.
8 devices in a mesh: member: 1 (over z), ty: 2 (over y), tx: 2 (over x), panel: 2 (over core).
Axes of the slice: x: 2, y: 2, z: 1, core: 2. Of those that a mesh axis runs over, the one named last changes fastest.
Arguments:
- tracer: float32 [6, 180, 180], P(('member', 'panel'), 'tx', 'ty')
- wind_a: float32 [6, 180, 180], P('panel', 'tx', 'ty')
- wind_b: float32 [6, 180, 180], P('panel', 'tx', 'ty')
- wind_scale: float32 [256], replicated
Outputs:
- output: float32 [6, 180, 180], P(('member', 'panel'), 'tx', 'ty')
All inputs are finite; a program needn't handle non-finite values.
Results may differ from a plain program's by a relative error of at most 0.001.
Values sent between devices are 32-bit elements.
A program may use at most 1 GiB of HBM per device.

v0:
```python
import math
import jax
import jax.numpy as jnp
from jax import lax
from jax.sharding import PartitionSpec as P

C_SPEED = 2.5
CFL_STEP = 0.12
EDGE_TABLE = (
    ((3, 1, 0), (1, 0, 0), (5, 3, 0), (4, 2, 0)),
    ((0, 1, 0), (2, 0, 0), (5, 1, 1), (4, 1, 0)),
    ((1, 1, 0), (3, 0, 0), (5, 2, 1), (4, 3, 1)),
    ((2, 1, 0), (0, 0, 0), (5, 0, 0), (4, 0, 1)),
    ((3, 3, 1), (1, 3, 0), (0, 3, 0), (2, 3, 1)),
    ((3, 2, 0), (1, 2, 1), (2, 2, 1), (0, 2, 0)),
)


def edge_sign(side_id, edge_id):
    out_sign = 1.0 if edge_id in (1, 3) else -1.0
    return out_sign if side_id in (0, 2) else -out_sign


def out_strips(field_a, field_b):
    return (field_a[:, 0:2, :],
            jnp.flip(field_a[:, -2:, :], axis=1),
            jnp.swapaxes(field_b[:, :, 0:2], 1, 2),
            jnp.swapaxes(jnp.flip(field_b[:, :, -2:], axis=2), 1, 2))


def to_blocks(ghosts):
    return (jnp.flip(ghosts[0], axis=1), ghosts[1],
            jnp.swapaxes(jnp.flip(ghosts[2], axis=1), 1, 2), jnp.swapaxes(ghosts[3], 1, 2))


def extend_field(field_now, blocks):
    return (jnp.concatenate([blocks[0], field_now, blocks[1]], axis=1),
            jnp.concatenate([blocks[2], field_now, blocks[3]], axis=2))


def wind_faces(blocks, wind_a, wind_b):
    ext_a = jnp.concatenate([blocks[0][:, 1:2, :], wind_a, blocks[1][:, 0:1, :]], axis=1)
    ext_b = jnp.concatenate([blocks[2][:, :, 1:2], wind_b, blocks[3][:, :, 0:1]], axis=2)
    return 0.5 * (ext_a[:, :-1, :] + ext_a[:, 1:, :]), 0.5 * (ext_b[:, :, :-1] + ext_b[:, :, 1:])


def face_flux_div(ext_arr, wind_face, step_scale, axis_id):
    face_count = ext_arr.shape[axis_id] - 3
    far_left = lax.slice_in_dim(ext_arr, 0, face_count, axis=axis_id)
    near_left = lax.slice_in_dim(ext_arr, 1, face_count + 1, axis=axis_id)
    near_right = lax.slice_in_dim(ext_arr, 2, face_count + 2, axis=axis_id)
    far_right = lax.slice_in_dim(ext_arr, 3, face_count + 3, axis=axis_id)
    face_val = (7.0 * (near_left + near_right) - (far_left + far_right)) / 12.0
    face_flux = step_scale * wind_face * face_val - (0.5 * C_SPEED) * (near_right - near_left)
    return (lax.slice_in_dim(face_flux, 1, face_count, axis=axis_id)
            - lax.slice_in_dim(face_flux, 0, face_count - 1, axis=axis_id))


def tendency(ext_a, ext_b, face_a, face_b, step_scale, inv_area):
    div_total = face_flux_div(ext_a, face_a, step_scale, 1) + face_flux_div(ext_b, face_b, step_scale, 2)
    return -div_total * inv_area


def inverse_area(row_ids, col_ids, cells):
    dalpha = 0.5 * math.pi / cells
    tan_a = jnp.tan((row_ids.astype(jnp.float32) + 0.5) * dalpha - 0.25 * math.pi)[:, None]
    tan_b = jnp.tan((col_ids.astype(jnp.float32) + 0.5) * dalpha - 0.25 * math.pi)[None, :]
    r_sq = 1.0 + tan_a * tan_a + tan_b * tan_b
    sqrt_g = (1.0 + tan_a * tan_a) * (1.0 + tan_b * tan_b) / (r_sq * jnp.sqrt(r_sq))
    return 1.0 / (dalpha * sqrt_g)


def solution(mesh):
    tile_count = mesh.shape['tx']
    panel_count = mesh.shape['panel']
    local_panels = 6 // panel_count
    group_axes = ('ty', 'tx', 'panel')
    field_spec = P(('member', 'panel'), 'tx', 'ty')
    wind_spec = P('panel', 'tx', 'ty')
    shift_up = [(idx_src, idx_src + 1) for idx_src in range(tile_count - 1)]
    shift_down = [(idx_src + 1, idx_src) for idx_src in range(tile_count - 1)]

    def device_id(panel_dev, tile_pos):
        return (tile_pos[1] * tile_count + tile_pos[0]) * panel_count + panel_dev

    def edge_tile(side_id, along_idx):
        last_idx = tile_count - 1
        return ((0, along_idx), (last_idx, along_idx), (along_idx, 0), (along_idx, last_idx))[side_id]

    cross_plan = []
    for panel_id in range(6):
        for side_id in range(4):
            src_panel, edge_id, flipped = EDGE_TABLE[panel_id][side_id]
            perm_pairs = []
            for along_idx in range(tile_count):
                src_along = tile_count - 1 - along_idx if flipped else along_idx
                perm_pairs.append((device_id(src_panel // local_panels, edge_tile(edge_id, src_along)),
                                   device_id(panel_id // local_panels, edge_tile(side_id, along_idx))))
            cross_plan.append((panel_id % local_panels, side_id, src_panel % local_panels, edge_id, flipped, perm_pairs))

    def fill_halo(field_a, field_b, signed):
        strips = out_strips(field_a, field_b)
        received = {}
        for slot_id, side_id, src_slot, edge_id, flipped, perm_pairs in cross_plan:
            one_strip = strips[edge_id][src_slot]
            if flipped:
                one_strip = jnp.flip(one_strip, axis=1)
            if signed:
                one_strip = edge_sign(side_id, edge_id) * one_strip
            moved_strip = lax.ppermute(one_strip, group_axes, perm_pairs)
            received[(side_id, slot_id)] = received.get((side_id, slot_id), 0.0) + moved_strip
        cross_blks = to_blocks([jnp.stack([received[(side_id, slot_id)] for slot_id in range(local_panels)])
                                for side_id in range(4)])
        own_blks = (lax.ppermute(field_a[:, -2:, :], 'tx', shift_up),
                    lax.ppermute(field_a[:, 0:2, :], 'tx', shift_down),
                    lax.ppermute(field_b[:, :, -2:], 'ty', shift_up),
                    lax.ppermute(field_b[:, :, 0:2], 'ty', shift_down))
        return tuple(own_blk + cross_blk for own_blk, cross_blk in zip(own_blks, cross_blks))

    def local_run(tracer, wind_a, wind_b, wind_scale):
        tile_rows = tracer.shape[1]
        tile_cols = tracer.shape[2]
        cells = tile_rows * tile_count
        time_step = CFL_STEP * (0.5 * math.pi / cells)
        row_ids = lax.axis_index('tx') * tile_rows + jnp.arange(tile_rows)
        col_ids = lax.axis_index('ty') * tile_cols + jnp.arange(tile_cols)
        inv_area = inverse_area(row_ids, col_ids, cells)
        face_a, face_b = wind_faces(fill_halo(wind_a, wind_b, True), wind_a, wind_b)

        def tend_of(tracer_now, step_scale):
            ext_a, ext_b = extend_field(tracer_now, fill_halo(tracer_now, tracer_now, False))
            return tendency(ext_a, ext_b, face_a, face_b, step_scale, inv_area)

        def one_step(step_id, tracer_now):
            step_scale = wind_scale[step_id]
            stage_one = tracer_now + time_step * tend_of(tracer_now, step_scale)
            stage_two = stage_one + time_step * tend_of(stage_one, step_scale)
            return 0.5 * (tracer_now + stage_two)

        return lax.fori_loop(0, wind_scale.shape[0], one_step, tracer)

    return jax.shard_map(local_run, mesh=mesh, in_specs=(field_spec, wind_spec, wind_spec, P()),
                         out_specs=field_spec, check_vma=False)
```

profile of v0, /device:TPU:0, one launch (start us, length us, event | category | flops | bytes accessed | tf_op | source)
XLA Modules:
  0.0 30156.6 jit_solution(16395495606265716705)
XLA Ops:
  52.4 30103.5 %while.14 = (s32[]{:T(128)}, f32[3,90,90]{2,1,0:T(8,128)S(1)}, f32[256]{0:T(256)S(1)}, f32[3,91,90]{2,1,0:T(8,128)S(1)}, f32[3,90,91]{2,1,0:T(8,128)S(1)}, /*ind...) while((s32[]{:T(128)}, f32[3,90,90]{2,1,0:T(8,128)S(1)}, f32[256]{0:T(256)S(1)}, ...), condition=%wide.region_1.2_spmd.clone, body=%wide.region_0.1_spmd.clone.sunk | while | flops 1830602 | bytes 3233369 | solution.py:140
  221.6 5.6 collective-permute-start.35
  456.8 5.6 collective-permute-start.35
  574.4 5.6 collective-permute-start.35
  692.0 5.6 collective-permute-start.35
  809.6 5.6 collective-permute-start.35
  1044.8 5.6 collective-permute-start.35
  1162.4 5.6 collective-permute-start.35
  1280.0 5.6 collective-permute-start.35
  1632.8 5.6 collective-permute-start.35
  1750.4 5.6 collective-permute-start.35
  1868.0 5.6 collective-permute-start.35
  2103.2 5.6 collective-permute-start.35
  2220.8 5.6 collective-permute-start.35
  2338.4 5.6 collective-permute-start.35
  2456.0 5.6 collective-permute-start.35
  2691.2 5.6 collective-permute-start.35
  2808.8 5.6 collective-permute-start.35
  2926.4 5.6 collective-permute-start.35
  3043.9 5.6 collective-permute-start.35
  3279.1 5.6 collective-permute-start.35
  3396.7 5.6 collective-permute-start.35
  3514.3 5.6 collective-permute-start.35
  3867.1 5.6 collective-permute-start.35
  3984.7 5.6 collective-permute-start.35
  4102.3 5.6 collective-permute-start.35
  4337.5 5.6 collective-permute-start.35
  4455.1 5.6 collective-permute-start.35
  4572.7 5.6 collective-permute-start.35
  4690.3 5.6 collective-permute-start.35
  4925.5 5.6 collective-permute-start.35
  5043.1 5.6 collective-permute-start.35
  5160.7 5.6 collective-permute-start.35
  5278.3 5.6 collective-permute-start.35
  5513.5 5.6 collective-permute-start.35
  5631.1 5.6 collective-permute-start.35
  5748.7 5.6 collective-permute-start.35
  6101.5 5.6 collective-permute-start.35
  6219.1 5.6 collective-permute-start.35
  6336.6 5.6 collective-permute-start.35
  6571.8 5.6 collective-permute-start.35
  6689.4 5.6 collective-permute-start.35
  6807.0 5.6 collective-permute-start.35
  6924.6 5.6 collective-permute-start.35
  7159.8 5.6 collective-permute-start.35
  7277.4 5.6 collective-permute-start.35
  7395.0 5.6 collective-permute-start.35
  7512.6 5.6 collective-permute-start.35
  7747.8 5.6 collective-permute-start.35
  7865.4 5.6 collective-permute-start.35
  7983.0 5.6 collective-permute-start.35
  8335.8 5.6 collective-permute-start.35
  8453.4 5.6 collective-permute-start.35
  8571.0 5.6 collective-permute-start.35
  8806.2 5.6 collective-permute-start.35
  8923.8 5.6 collective-permute-start.35
  9041.4 5.6 collective-permute-start.35
  9159.0 5.6 collective-permute-start.35
  9394.2 5.6 collective-permute-start.35
  9511.7 5.6 collective-permute-start.35
  9629.3 5.6 collective-permute-start.35
  9746.9 5.6 collective-permute-start.35
  9982.1 5.6 collective-permute-start.35
  10099.7 5.6 collective-permute-start.35
  (53047 shorter events, 29486.8 us)
Async XLA Ops:
  221.6 62.8 collective-permute-start.35
  339.2 62.8 collective-permute-start.35
  456.8 62.8 collective-permute-start.35
  574.4 62.8 collective-permute-start.35
  692.0 62.8 collective-permute-start.35
  809.6 62.8 collective-permute-start.35
  927.2 62.8 collective-permute-start.35
  1044.8 62.8 collective-permute-start.35
  1162.4 62.8 collective-permute-start.35
  1280.0 62.8 collective-permute-start.35
  1397.6 62.8 collective-permute-start.35
  1515.2 62.8 collective-permute-start.35
  1632.8 62.8 collective-permute-start.35
  1750.4 62.8 collective-permute-start.35
  1868.0 62.8 collective-permute-start.35
  1985.6 62.8 collective-permute-start.35
  2103.2 62.8 collective-permute-start.35
  2220.8 62.8 collective-permute-start.35
  2338.4 62.8 collective-permute-start.35
  2456.0 62.8 collective-permute-start.35
  2573.6 62.8 collective-permute-start.35
  2691.2 62.8 collective-permute-start.35
  2808.8 62.8 collective-permute-start.35
  2926.4 62.8 collective-permute-start.35
  3043.9 62.8 collective-permute-start.35
  3161.5 62.8 collective-permute-start.35
  3279.1 62.8 collective-permute-start.35
  3396.7 62.8 collective-permute-start.35
  3514.3 62.8 collective-permute-start.35
  3631.9 62.8 collective-permute-start.35
  3749.5 62.8 collective-permute-start.35
  3867.1 62.8 collective-permute-start.35
  3984.7 62.8 collective-permute-start.35
  4102.3 62.8 collective-permute-start.35
  4219.9 62.8 collective-permute-start.35
  4337.5 62.8 collective-permute-start.35
  4455.1 62.8 collective-permute-start.35
  4572.7 62.8 collective-permute-start.35
  4690.3 62.8 collective-permute-start.35
  4807.9 62.8 collective-permute-start.35
  4925.5 62.8 collective-permute-start.35
  5043.1 62.8 collective-permute-start.35
  5160.7 62.8 collective-permute-start.35
  5278.3 62.8 collective-permute-start.35
  5395.9 62.8 collective-permute-start.35
  5513.5 62.8 collective-permute-start.35
  5631.1 62.8 collective-permute-start.35
  5748.7 62.8 collective-permute-start.35
  5866.3 62.8 collective-permute-start.35
  5983.9 62.8 collective-permute-start.35
  6101.5 62.8 collective-permute-start.35
  6219.1 62.8 collective-permute-start.35
  6336.6 62.8 collective-permute-start.35
  6454.2 62.8 collective-permute-start.35
  6571.8 62.8 collective-permute-start.35
  6689.4 62.8 collective-permute-start.35
  6807.0 62.8 collective-permute-start.35
  6924.6 62.8 collective-permute-start.35
  7042.2 62.8 collective-permute-start.35
  7159.8 62.8 collective-permute-start.35
  7277.4 62.8 collective-permute-start.35
  7395.0 62.8 collective-permute-start.35
  7512.6 62.8 collective-permute-start.35
  7630.2 62.8 collective-permute-start.35
  (14305 other events, 125233.1 us)
where the time goes:
time: 30400 us; the launch traced here: 30200 us
  starting transfers between devices  22200 us (73%)
  waiting for transfers between devices  5550 us (18%)
  local copies, waits for them, and re-layouts  1080 us (4%)
  other arithmetic  1060 us (3%)
  loops' own time  318 us (1%)
    ppermute x12312, starting transfers between devices, fill_halo(): moved_strip = lax.ppermute(one_strip, group_axes, perm_pairs)  15700 us
    ppermute x12312, waiting for transfers between devices, fill_halo(): moved_strip = lax.ppermute(one_strip, group_axes, perm_pairs)  5550 us
    ppermute x513, starting transfers between devices, fill_halo(): lax.ppermute(field_b[:, :, -2:], 'ty', shift_up)  2770 us
    ppermute x513, starting transfers between devices, fill_halo(): lax.ppermute(field_a[:, -2:, :], 'tx', shift_up)  2330 us
    sub x1024, other arithmetic, face_flux_div(): step_scale * wind_face * face_val - 0.5 * C_SPEED * (near_right - near_left)  895 us
    ppermute x513, starting transfers between devices, fill_halo(): lax.ppermute(field_a[:, 0:2, :], 'tx', shift_down)  663 us
    ppermute x513, starting transfers between devices, fill_halo(): lax.ppermute(field_b[:, :, 0:2], 'ty', shift_down)  657 us

commit v1 on v0

v1 whole, which is shorter than its diff:
```python
import functools
import math

import jax
import jax.numpy as jnp
import numpy as np
from jax import lax
from jax.experimental import pallas as pl
from jax.experimental.pallas import tpu as pltpu
from jax.sharding import PartitionSpec as P

C_SPEED = 2.5
CFL_STEP = 0.12
MESH = pl.DeviceIdType.MESH
HIGHEST = lax.Precision.HIGHEST

TWIN = (1, 0, 3, 2, 5, 4)
ACROSS = (2, 4, 0, 5, 1, 3)
PRIMARY = (0, 2, 4)

SIZE = 128
TILES = 16
LOW = 6
OWN = 90
BLOCK_STEPS = 8


def pos_idx(pos):
    return TILES * (pos % 8) + pos // 8


def tiles_of(arr):
    return [arr[8 * i:8 * i + 8] for i in range(TILES)]


def join(tiles):
    return jnp.concatenate(tiles, axis=0)


def roll_rows(tile, shift):
    return pltpu.roll(tile, shift % 8, 0)


def solution(mesh):
    axis_names = mesh.axis_names

    def local_run(tracer, wind_a, wind_b, wind_scale):
        own = tracer.shape[1]
        cells = 2 * own
        steps = wind_scale.shape[0]
        dalpha = 0.5 * math.pi / cells
        tan_u = np.tan((pos_idx(np.arange(SIZE)) - LOW + 0.5) * dalpha - 0.25 * math.pi)
        tan_a, tan_b = tan_u[:, None], tan_u[None, :]
        r_sq = 1.0 + tan_a * tan_a + tan_b * tan_b
        inv_sqrt_g = r_sq * np.sqrt(r_sq) / ((1.0 + tan_a * tan_a) * (1.0 + tan_b * tan_b))
        gain = (0.5 * C_SPEED * CFL_STEP * inv_sqrt_g).astype(np.float32)
        out = pl.pallas_call(
            functools.partial(kernel, own, steps, axis_names),
            out_shape=jax.ShapeDtypeStruct(tracer.shape, jnp.float32),
            in_specs=[pl.BlockSpec(memory_space=pltpu.SMEM)] + [pl.BlockSpec(memory_space=pltpu.VMEM)] * 4,
            out_specs=pl.BlockSpec(memory_space=pltpu.VMEM),
            scratch_shapes=[
                pltpu.VMEM((6, SIZE, SIZE), jnp.float32),
                pltpu.VMEM((6, SIZE, SIZE), jnp.float32),
                pltpu.VMEM((6, SIZE, SIZE), jnp.float32),
                pltpu.VMEM((6, SIZE, SIZE), jnp.float32),
                pltpu.VMEM((SIZE, SIZE), jnp.float32),
                pltpu.VMEM((3, 3, own, own), jnp.float32),
                pltpu.VMEM((3, own, own), jnp.float32),
                pltpu.VMEM((6, 32, SIZE), jnp.float32),
                pltpu.VMEM((2, 6, 32, SIZE), jnp.float32),
                pltpu.VMEM((3, 8, SIZE), jnp.float32),
                pltpu.VMEM((2, 3, 8, SIZE), jnp.float32),
                pltpu.SemaphoreType.DMA((2, 9)),
                pltpu.SemaphoreType.DMA((2, 9)),
                pltpu.SemaphoreType.DMA((3, 3)),
                pltpu.SemaphoreType.DMA((3, 3)),
                pltpu.SemaphoreType.DMA((3,)),
                pltpu.SemaphoreType.DMA((3,)),
            ],
            name="advect",
        )(wind_scale, tracer, wind_a, wind_b, gain)
        return out

    field_spec = P(('member', 'panel'), 'tx', 'ty')
    wind_spec = P('panel', 'tx', 'ty')
    return jax.shard_map(local_run, mesh=mesh, in_specs=(field_spec, wind_spec, wind_spec, P()),
                         out_specs=field_spec, check_vma=False)


def kernel(own, steps, axis_names, ws_ref, q_in, wa_in, wb_in, gain_ref, out_ref,
           qa, qb, wl, wf, keep, tiles, result, send, recv, csend, crecv,
           ssem, rsem, tsend, trecv, osend, orecv):
    tx, ty, core = lax.axis_index('tx'), lax.axis_index('ty'), lax.axis_index('panel')

    def at(bx, by, bz):
        place = {'tx': bx, 'ty': by, 'panel': lax.rem(bz + bx, 2)}
        return {name: place.get(name, 0) for name in axis_names}

    bx, by, bz = tx, ty, lax.rem(core + tx, 2)
    is_first = core == 0

    def pick(first, second):
        return jnp.where(is_first, first, second)

    homes = (
        (pick(1, tx), pick(tx, 0), ty, pick(0, 1)),
        (pick(1 - tx, 1 - ty), pick(1, tx), pick(ty, 1), pick(1, 2)),
        (pick(0, ty), pick(1 - tx, tx), pick(ty, 0), pick(0, 2)),
    )
    fields = (q_in, wa_in, wb_in)
    for slot in range(3):
        ox, oy, oz, quad = homes[slot]
        mine = (ox == bx) & (oy == by) & (oz == bz)

        @pl.when(mine)
        def _():
            for f in range(3):
                tiles[f, quad] = fields[f][slot]

        @pl.when(jnp.logical_not(mine))
        def _():
            for f in range(3):
                pltpu.make_async_remote_copy(
                    fields[f].at[slot], tiles.at[f, quad], tsend.at[f, slot], trecv.at[f, quad],
                    device_id=at(ox, oy, oz), device_id_type=MESH).start()

    def owner(kx, ky, kc):
        return {name: {'tx': kx, 'ty': ky, 'panel': kc}.get(name, 0) for name in axis_names}

    flip_a = (1 - lax.rem(bx + by, 2), lax.rem(bx + by, 2), by)
    flip_b = (bz, bz, jnp.where(bz == 1, 1 - bx, bx))
    panel = (jnp.where(bx == 1, 0, 2), jnp.where(by == 1, 1, 3), jnp.where(bz == 1, 4, 5))
    for slot in range(3):
        ox, oy, oz, quad = homes[slot]
        mine = (ox == bx) & (oy == by) & (oz == bz)

        @pl.when(jnp.logical_not(mine))
        def _():
            for f in range(3):
                pltpu.make_async_remote_copy(
                    fields[f].at[slot], tiles.at[f, quad], tsend.at[f, slot], trecv.at[f, quad],
                    device_id=at(ox, oy, oz), device_id_type=MESH).wait_send()
    for quad in range(3):
        from_core = panel[quad] // 3
        stays = (flip_a[quad] == tx) & (flip_b[quad] == ty) & (from_core == core)

        @pl.when(jnp.logical_not(stays))
        def _():
            for f in range(3):
                pltpu.make_async_remote_copy(
                    fields[f].at[0], tiles.at[f, quad], tsend.at[f, 0], trecv.at[f, quad],
                    device_id=owner(flip_a[quad], flip_b[quad], from_core), device_id_type=MESH).wait_recv()

    pos_r = lax.broadcasted_iota(jnp.int32, (SIZE, own), 0)
    cell_c = lax.broadcasted_iota(jnp.int32, (SIZE, own), 1)
    cell_r = lax.broadcasted_iota(jnp.int32, (own, SIZE), 0)
    pos_c = lax.broadcasted_iota(jnp.int32, (own, SIZE), 1)

    def spot(pos, flip):
        dist = TILES * lax.rem(pos, 8) + pos // 8 - LOW
        inside = (dist >= 0) & (dist < own)
        return jnp.where(inside, jnp.where(flip == 1, own - 1 - dist, dist), -1)

    def place_rows(flip):
        return jnp.where(spot(pos_r, flip) == cell_c, 1.0, 0.0)

    def place_cols(flip):
        return jnp.where(spot(pos_c, flip) == cell_r, 1.0, 0.0)

    def dot(lhs, rhs):
        return jnp.dot(lhs, rhs, precision=HIGHEST, preferred_element_type=jnp.float32)

    for quad in range(3):
        rows, cols = place_rows(flip_a[quad]), place_cols(flip_b[quad])
        plain = (0, 2, 5)[quad]
        turned = TWIN[plain]
        sign_a = jnp.where(flip_a[quad] == 1, -1.0, 1.0)
        sign_b = jnp.where(flip_b[quad] == 1, -1.0, 1.0)
        q_loc = dot(dot(rows, tiles[0, quad]), cols)
        a_loc = sign_a * dot(dot(rows, tiles[1, quad]), cols)
        b_loc = sign_b * dot(dot(rows, tiles[2, quad]), cols)
        qa[plain] = q_loc
        qa[turned] = q_loc.T
        qb[plain] = a_loc
        qb[turned] = b_loc.T
        wl[plain] = b_loc
        wl[turned] = a_loc.T

    sub = lax.broadcasted_iota(jnp.int32, (8, SIZE), 0)
    lane = lax.broadcasted_iota(jnp.int32, (8, SIZE), 1)
    halo_rows = sub >= 6
    halo_lanes = lax.rem(lane, 8) >= 6
    first_row = sub == 0

    def take(tile, idx, axis):
        return jnp.take_along_axis(tile, idx, axis=axis, mode="promise_in_bounds")

    sides = ((0, 0, 1), (1, 0, 0), (0, 1, 0), (1, 0, 1), (0, 1, 1), (1, 1, 0))
    strip_axis = (1, 2, 0, 2, 0, 1)
    place_in = (2, 4, 0, 5, 1, 3)
    axis_first = (0, 2, 4)
    axis_flip = ((1, 0, 0), (0, 1, 0), (0, 0, 1))
    corner_flip = {0: (0, 1, 1), 2: (1, 0, 1), 4: (1, 1, 0)}

    def peer(flip):
        return at(*(1 - b if f else b for b, f in zip((bx, by, bz), flip)))

    def copies(slot):
        made = []
        for axis in (1, 0, 2):
            first = axis_first[axis]
            made.append(pltpu.make_async_remote_copy(
                send.at[pl.ds(first, 2)], recv.at[slot, pl.ds(first, 2)], ssem.at[slot, axis], rsem.at[slot, axis],
                device_id=peer(axis_flip[axis]), device_id_type=MESH))
        for n, arr in enumerate(PRIMARY):
            made.append(pltpu.make_async_remote_copy(
                csend.at[n], crecv.at[slot, n], ssem.at[slot, 3 + n], rsem.at[slot, 3 + n],
                device_id=peer(corner_flip[arr]), device_id_type=MESH))
        return made

    row_perm = 5 - lax.rem(sub, 2)
    lane_perm = 125 - 8 * (lane // 8) - lax.rem(lane, 2)
    row_pair = sub // 2
    lane_pair = lax.rem(lane, 8) // 2

    def by_pair(pair, parts):
        res = parts[3]
        for m in (2, 1, 0):
            res = jnp.where(pair == m, parts[m], res)
        return res

    def exchange(arrs, twins, slot, row_sign, corner_sign):
        for k in range(6):
            a = tiles_of(arrs[k])
            msg = [by_pair(row_pair, [take(a[15 - 4 * j - m], row_perm, 0) for m in range(4)]) for j in range(4)]
            send[place_in[k]] = row_sign * jnp.concatenate(msg, axis=0)
            if k in PRIMARY:
                csend[PRIMARY.index(k)] = corner_sign * by_pair(lane_pair, [take(t, lane_perm, 1) for t in msg])
        made = copies(slot)
        for c in made:
            c.start()
        for c in made:
            c.wait()
        for k in range(6):
            a = tiles_of(arrs[k])
            msg = tiles_of_strip(recv[slot, place_in[k]])
            if k in PRIMARY:
                corner = crecv[slot, PRIMARY.index(k)]
                msg = [jnp.where(halo_lanes, pltpu.roll(corner, (6 - 2 * j) % 128, 1), msg[j]) for j in range(4)]
            arrs[k] = join([jnp.where(halo_rows, roll_rows(msg[i // 4], 6 - 2 * (i % 4)), a[i]) for i in range(TILES)])

    def tiles_of_strip(arr):
        return [arr[8 * j:8 * j + 8] for j in range(4)]

    own_rows_halo_lanes = halo_lanes & jnp.logical_not(halo_rows)

    def fill_lanes(arrs, twins):
        for k in PRIMARY:
            t = TWIN[k]
            from_twin = tiles_of(twins[t].T)
            from_self = tiles_of(twins[k].T) if twins is not arrs else tiles_of(arrs[k].T)
            mine, other = tiles_of(arrs[k]), tiles_of(arrs[t])
            new_mine = join([jnp.where(own_rows_halo_lanes, from_twin[i], mine[i]) for i in range(TILES)])
            new_other = join([jnp.where(halo_lanes, from_self[i], other[i]) for i in range(TILES)])
            arrs[k] = new_mine
            arrs[t] = new_other

    def set_ghosts(arrs, new):
        for k in range(6):
            near = new[ACROSS[k]]
            arrs[k, 32:33] = near[56:57]
            arrs[k, 40:41] = near[48:49]

    exchange(qb, wl, 0, -1.0, -1.0)
    exchange(wl, qb, 1, 1.0, -1.0)
    for k in PRIMARY:
        t = TWIN[k]
        lane_k, lane_t = tiles_of(wl[t].T), tiles_of(wl[k].T)
        mine, other = tiles_of(qb[k]), tiles_of(qb[t])
        qb[k] = join([jnp.where(own_rows_halo_lanes, lane_k[i], mine[i]) for i in range(TILES)])
        qb[t] = join([jnp.where(halo_lanes, lane_t[i], other[i]) for i in range(TILES)])
    for k in range(6):
        qb[k, 40:41] = -qb[ACROSS[k], 48:49]
    for k in range(6):
        a = tiles_of(qb[k])
        nxt = a[1:] + [roll_rows(a[0], -1)]
        wf[k] = (0.5 / (6.0 * C_SPEED)) * (qb[k] + join(nxt))
    keep[...] = 1.0 - 4.0 * gain_ref[...]

    def x_part(a_ref, k, faces):
        a = a_ref[k]
        before = jnp.concatenate([a_ref[k, 119:127], a[:120]], axis=0)
        after = jnp.concatenate([a[8:], a_ref[k, 1:9]], axis=0)
        m = before + after
        v = 8.0 * a - m
        v_after = jnp.concatenate([v[8:], roll_rows(v[:8], -1)], axis=0)
        flux = faces * (v + v_after)
        flux_before = jnp.concatenate([roll_rows(flux[120:], 1), flux[:120]], axis=0)
        return (m - flux) + flux_before

    def stage(src, dst, second, scale):
        gain = gain_ref[...]
        ready = []
        for k in PRIMARY:
            t = TWIN[k]
            parts = []
            for j in (k, t):
                if second:
                    faces = wl[j]
                else:
                    faces = scale * wf[j]
                    wl[j] = faces
                x = x_part(src, j, faces)
                if second:
                    x = (0.5 * gain) * x
                else:
                    x = gain * x
                if j == k:
                    if second:
                        x = (0.5 * dst[k] + (0.5 * keep[...]) * src[k]) + x
                    else:
                        x = keep[...] * src[k] + x
                parts.append(x)
            ready.append(parts)
        new = [None] * 6
        for k, (zk, zt) in zip(PRIMARY, ready):
            new[k] = zk + zt.T
            new[TWIN[k]] = zt + zk.T
        for k in range(6):
            dst[k] = new[k]
        set_ghosts(dst, new)

    block_count = steps // BLOCK_STEPS

    def block(blk, carry):
        slot = lax.rem(blk, 2)
        exchange(qa, qa, slot, 1.0, 1.0)
        fill_lanes(qa, qa)
        for k in range(6):
            near = ACROSS[k]
            qa[k, 32:33] = qa[near, 56:57]
            qa[k, 40:41] = qa[near, 48:49]

        def one_step(step, inner):
            scale = ws_ref[blk * BLOCK_STEPS + step]
            stage(qa, qb, False, scale)
            stage(qb, qa, True, scale)
            return inner

        lax.fori_loop(0, BLOCK_STEPS, one_step, 0)
        return carry

    lax.fori_loop(0, block_count, block, 0)

    for quad in range(3):
        plain = (0, 2, 5)[quad]
        rows, cols = place_cols(flip_a[quad]), place_rows(flip_b[quad])
        result[quad] = dot(dot(rows, qa[plain]), cols)
    for quad in range(3):
        from_core, from_slot = panel[quad] // 3, lax.rem(panel[quad], 3)
        stays = (flip_a[quad] == tx) & (flip_b[quad] == ty) & (from_core == core)

        @pl.when(stays)
        def _():
            out_ref[from_slot] = result[quad]

        @pl.when(jnp.logical_not(stays))
        def _():
            pltpu.make_async_remote_copy(
                result.at[quad], out_ref.at[from_slot], osend.at[quad], orecv.at[from_slot],
                device_id=owner(flip_a[quad], flip_b[quad], from_core), device_id_type=MESH).start()
    for quad in range(3):
        from_core, from_slot = panel[quad] // 3, lax.rem(panel[quad], 3)
        stays = (flip_a[quad] == tx) & (flip_b[quad] == ty) & (from_core == core)

        @pl.when(jnp.logical_not(stays))
        def _():
            pltpu.make_async_remote_copy(
                result.at[quad], out_ref.at[from_slot], osend.at[quad], orecv.at[from_slot],
                device_id=owner(flip_a[quad], flip_b[quad], from_core), device_id_type=MESH).wait_send()
    for slot in range(3):
        ox, oy, oz, quad = homes[slot]
        mine = (ox == bx) & (oy == by) & (oz == bz)

        @pl.when(jnp.logical_not(mine))
        def _():
            pltpu.make_async_remote_copy(
                result.at[0], out_ref.at[slot], osend.at[0], orecv.at[slot],
                device_id=at(ox, oy, oz), device_id_type=MESH).wait_recv()
```

time: 30400 us -> 238 us (0.01)
  starting transfers between devices: 22200 us -> 0 us
  waiting for transfers between devices: 5550 us -> 0 us
  local copies, waits for them, and re-layouts: 1080 us -> 1.58 us
  other arithmetic: 1060 us -> 0 us
  loops' own time: 318 us -> 0 us
    ppermute x14364 -> x0, starting transfers between devices: 22200 us -> none  [the longest x12312 15700 us: fill_halo(): moved_strip = lax.ppermute(one_strip, group_axes, perm_pairs)]
    ppermute x14364 -> x0, waiting for transfers between devices: 5550 us -> none  [the longest x12312 5550 us: fill_halo(): moved_strip = lax.ppermute(one_strip, group_axes, perm_pairs)]
    sub x1024 -> x0, other arithmetic: 895 us -> none  [face_flux_div(): step_scale * wind_face * face_val - 0.5 * C_SPEED * (near_right - near_left)]
    rev x5130 -> x0, local copies, waits for them, and re-layouts: 381 us -> none  [the longest x3591 217 us: fill_halo(): one_strip = jnp.flip(one_strip, axis=1)]
    another operation x1 -> x0, loops' own time: 318 us -> none  [local_run(): return lax.fori_loop(0, wind_scale.shape[0], one_step, tracer)]
where the time goes in v1:
time: 238 us
  Pallas kernels  236 us (99%)
    pallas_call x1, Pallas kernels, local_run(): pl.pallas_call(functools.partial(kernel, own, steps, axis_names), out_sha...  236 us

profile of v1, /device:TPU:0, one launch (start us, length us, event | category | flops | bytes accessed | tf_op | source)
XLA Modules:
  0.0 238.0 jit_solution(5311441275860396364)
XLA Ops:
  0.0 236.4 %advect.1 = f32[3,90,90]{2,1,0:T(8,128)} custom-call(f32[256]{0:T(256)} %ws_ref.1, f32[3,90,90]{2,1,0:T(8,128)} %q_in.1, f32[3,90,90]{2,1,0:T(8,128)} %wa_in.1, f32[3,90,90]{2,1,0:T(8,128)} %wb_in.1, f32[128,128]{1,0:T(8,128)} %constant.2.clone.gain_ref), custom_call_target="tpu_custom_call" | custom-call | tf_op jit(solution)/shard_map/advect/pallas_call | solution.py:57
  236.5 1.6 copy.7

commit v2 on v1

v2 whole, which is shorter than its diff:
```python
import functools
import math

import jax
import jax.numpy as jnp
import numpy as np
from jax import lax
from jax.experimental import pallas as pl
from jax.experimental.pallas import tpu as pltpu
from jax.sharding import PartitionSpec as P

C_SPEED = 2.5
CFL_STEP = 0.12
MESH = pl.DeviceIdType.MESH
HIGHEST = lax.Precision.HIGHEST

TWIN = (1, 0, 3, 2, 5, 4)
ACROSS = (2, 4, 0, 5, 1, 3)
PRIMARY = (0, 2, 4)
STRIPS = ((2, 4), (0, 5), (1, 3))
CORNERS = {0: ((0, 1, 1), 1, 0), 2: ((1, 0, 1), 0, 0), 4: ((1, 1, 0), 0, 1)}

SIZE = 128
TILES = 16
LOW = 2
OWN = 90
BLOCK_STEPS = 9


def pos_idx(pos):
    return TILES * (pos % 8) + pos // 8


def tiles_of(arr):
    return [arr[8 * i:8 * i + 8] for i in range(arr.shape[0] // 8)]


def join(tiles):
    return jnp.concatenate(tiles, axis=0)


def roll_rows(tile, shift):
    return pltpu.roll(tile, shift % 8, 0)


def solution(mesh):
    axis_names = mesh.axis_names

    def local_run(tracer, wind_a, wind_b, wind_scale):
        own = tracer.shape[1]
        cells = 2 * own
        steps = wind_scale.shape[0]
        dalpha = 0.5 * math.pi / cells
        tan_u = np.tan((pos_idx(np.arange(SIZE)) - LOW + 0.5) * dalpha - 0.25 * math.pi)
        tan_a, tan_b = tan_u[:, None], tan_u[None, :]
        r_sq = 1.0 + tan_a * tan_a + tan_b * tan_b
        inv_sqrt_g = r_sq * np.sqrt(r_sq) / ((1.0 + tan_a * tan_a) * (1.0 + tan_b * tan_b))
        gain = (0.5 * C_SPEED * CFL_STEP * inv_sqrt_g).astype(np.float32)
        out = pl.pallas_call(
            functools.partial(kernel, own, steps, axis_names),
            out_shape=jax.ShapeDtypeStruct(tracer.shape, jnp.float32),
            in_specs=[pl.BlockSpec(memory_space=pltpu.SMEM)] + [pl.BlockSpec(memory_space=pltpu.VMEM)] * 4,
            out_specs=pl.BlockSpec(memory_space=pltpu.VMEM),
            scratch_shapes=[
                pltpu.VMEM((6, SIZE, SIZE), jnp.float32),
                pltpu.VMEM((6, SIZE, SIZE), jnp.float32),
                pltpu.VMEM((BLOCK_STEPS, 6, SIZE, SIZE), jnp.float32),
                pltpu.VMEM((6, SIZE, SIZE), jnp.float32),
                pltpu.VMEM((4, SIZE, SIZE), jnp.float32),
                pltpu.VMEM((3, 3, own, own), jnp.float32),
                pltpu.VMEM((3, own, own), jnp.float32),
                pltpu.VMEM((3, 3, 72, SIZE), jnp.float32),
                pltpu.VMEM((4, 3, 72, SIZE), jnp.float32),
                pltpu.VMEM((3, 3, 16, SIZE), jnp.float32),
                pltpu.VMEM((4, 3, 16, SIZE), jnp.float32),
                pltpu.SemaphoreType.DMA((4, 6)),
                pltpu.SemaphoreType.DMA((4, 6)),
                pltpu.SemaphoreType.DMA((3, 3)),
                pltpu.SemaphoreType.DMA((3, 3)),
                pltpu.SemaphoreType.DMA((3,)),
                pltpu.SemaphoreType.DMA((3,)),
            ],
            name="advect",
        )(wind_scale, tracer, wind_a, wind_b, gain)
        return out

    field_spec = P(('member', 'panel'), 'tx', 'ty')
    wind_spec = P('panel', 'tx', 'ty')
    return jax.shard_map(local_run, mesh=mesh, in_specs=(field_spec, wind_spec, wind_spec, P()),
                         out_specs=field_spec, check_vma=False)


def kernel(own, steps, axis_names, ws_ref, q_in, wa_in, wb_in, gain_ref, out_ref,
           qa, qb, sw, wf, coef, tiles, result, send, recv, csend, crecv,
           ssem, rsem, tsend, trecv, osend, orecv):
    tx, ty, core = lax.axis_index('tx'), lax.axis_index('ty'), lax.axis_index('panel')
    by, bz, bx = tx, ty, lax.rem(core + tx + 1, 2)

    def place(kx, ky, kc):
        return {name: {'tx': kx, 'ty': ky, 'panel': kc}.get(name, 0) for name in axis_names}

    def at(ox, oy, oz):
        return place(oy, oz, lax.rem(ox + oy + 1, 2))

    def pick(first, second):
        return jnp.where(core == 0, first, second)

    homes = (
        (pick(1, tx), pick(tx, 0), ty, pick(0, 1)),
        (pick(1 - tx, 1 - ty), pick(1, tx), pick(ty, 1), pick(1, 2)),
        (pick(0, ty), pick(1 - tx, tx), pick(ty, 0), pick(0, 2)),
    )
    leaves = [jnp.logical_not((ox == bx) & (oy == by) & (oz == bz)) for ox, oy, oz, _ in homes]
    flip_a = (1 - lax.rem(bx + by, 2), lax.rem(bx + by, 2), by)
    flip_b = (bz, bz, jnp.where(bz == 1, 1 - bx, bx))
    panel = (jnp.where(bx == 1, 0, 2), jnp.where(by == 1, 1, 3), jnp.where(bz == 1, 4, 5))
    holder = [place(flip_a[n], flip_b[n], panel[n] // 3) for n in range(3)]
    slot_of = [lax.rem(panel[n], 3) for n in range(3)]
    comes = [jnp.logical_not((flip_a[n] == tx) & (flip_b[n] == ty) & (panel[n] // 3 == core)) for n in range(3)]

    fields = (q_in, wa_in, wb_in)

    def tile_copy(f, slot, quad, device):
        return pltpu.make_async_remote_copy(
            fields[f].at[slot], tiles.at[f, quad], tsend.at[f, slot], trecv.at[f, quad],
            device_id=device, device_id_type=MESH)

    for f in (1, 2, 0):
        for slot in range(3):
            ox, oy, oz, quad = homes[slot]

            @pl.when(leaves[slot])
            def _():
                tile_copy(f, slot, quad, at(ox, oy, oz)).start()

            @pl.when(jnp.logical_not(leaves[slot]))
            def _():
                tiles[f, quad] = fields[f][slot]

    pos_r = lax.broadcasted_iota(jnp.int32, (SIZE, own), 0)
    cell_c = lax.broadcasted_iota(jnp.int32, (SIZE, own), 1)
    cell_r = lax.broadcasted_iota(jnp.int32, (own, SIZE), 0)
    pos_c = lax.broadcasted_iota(jnp.int32, (own, SIZE), 1)

    def spot(pos, flip):
        dist = TILES * lax.rem(pos, 8) + pos // 8 - LOW
        inside = (dist >= 0) & (dist < own)
        return jnp.where(inside, jnp.where(flip == 1, own - 1 - dist, dist), -1)

    def place_rows(flip):
        return jnp.where(spot(pos_r, flip) == cell_c, 1.0, 0.0)

    def place_cols(flip):
        return jnp.where(spot(pos_c, flip) == cell_r, 1.0, 0.0)

    def dot(lhs, rhs):
        return jnp.dot(lhs, rhs, precision=HIGHEST, preferred_element_type=jnp.float32)

    PLAIN = (0, 2, 5)

    sub = lax.broadcasted_iota(jnp.int32, (8, SIZE), 0)
    lane = lax.broadcasted_iota(jnp.int32, (8, SIZE), 1)
    lane_s, lane_i = lax.rem(lane, 8), lane // 8
    halo_lane = (lane_s >= 6) | ((lane_s == 5) & (lane_i >= 12))
    mirror = jnp.where(lane_i < 8, 67, 194)
    pair_src = mirror - (8 * lane_i + 6 + lax.rem(lane, 2))
    edge_src = jnp.where(lane_i >= 12, 189 - 8 * lane_i, 0)
    halo_src = jnp.where(halo_lane, mirror - lane, 0)
    row_even, row_odd = 5 - lax.rem(sub, 2), 4 - lax.rem(sub, 2)
    row_pair, lane_pair = sub // 2, lane_s // 2

    def take(tile, idx, axis):
        return jnp.take_along_axis(tile, idx, axis=axis, mode="promise_in_bounds")

    def by_number(number, parts):
        res = parts[3]
        for m in (2, 1, 0):
            res = jnp.where(number == m, parts[m], res)
        return res

    def peer(mirrored):
        return at(*(1 - b if m else b for b, m in zip((bx, by, bz), mirrored)))

    def strip_copy(axis, out, slot):
        return pltpu.make_async_remote_copy(
            send.at[out, axis], recv.at[slot, axis], ssem.at[slot, axis], rsem.at[slot, axis],
            device_id=peer(tuple(int(n == axis) for n in range(3))), device_id_type=MESH)

    def corner_copy(k, out, slot):
        n = PRIMARY.index(k)
        return pltpu.make_async_remote_copy(
            csend.at[out, n], crecv.at[slot, n], ssem.at[slot, 3 + n], rsem.at[slot, 3 + n],
            device_id=peer(CORNERS[k][0]), device_id_type=MESH)

    def pack_strip(get, axis, out, sign):
        for n, k in enumerate(STRIPS[axis]):
            a = [get(k, i) for i in range(TILES)]
            for j in range(4):
                first, perm = (7, row_even) if j < 2 else (23, row_odd)
                part = by_number(row_pair, [take(a[first - 4 * j - m], perm, 0) for m in range(4)])
                send[out, axis, 32 * n + 8 * j:32 * n + 8 * j + 8] = sign * part if sign != 1.0 else part
            tail = by_number(lax.rem(sub, 4), [take(a[11 - m], row_even * 0 + 5, 0) for m in range(4)])
            tail = sign * tail if sign != 1.0 else tail
            send[out, axis, 64 + 4 * n:68 + 4 * n] = tail[4 * n:4 * n + 4]

    def pack_corner(k, out, sign):
        _, axis, n = CORNERS[k]
        msg = [send[out, axis, 32 * n + 8 * j:32 * n + 8 * j + 8] for j in range(4)]
        tail = send[out, axis, 64:72]
        pairs = by_number(lane_pair, [take(m, pair_src, 1) for m in msg])
        edges = by_number(lane_s, [take(m, edge_src, 1) for m in msg])
        rest = jnp.where(halo_lane, take(tail, halo_src, 1), edges)
        slot = PRIMARY.index(k)
        csend[out, slot, 0:8] = sign * pairs if sign != 1.0 else pairs
        csend[out, slot, 8:16] = sign * rest if sign != 1.0 else rest

    def start_all(arrs, out, slot, row_sign, corner_sign):
        def get(k, i):
            return arrs[k, 8 * i:8 * i + 8]
        pack_strip(get, 2, out, row_sign)
        strip_copy(2, out, slot).start()
        pack_strip(get, 1, out, row_sign)
        pack_corner(0, out, corner_sign)
        corner_copy(0, out, slot).start()
        pack_strip(get, 0, out, row_sign)
        pack_corner(4, out, corner_sign)
        corner_copy(4, out, slot).start()
        strip_copy(1, out, slot).start()
        pack_corner(2, out, corner_sign)
        corner_copy(2, out, slot).start()
        strip_copy(0, out, slot).start()

    def merge_corner(k, slot):
        _, axis, n = CORNERS[k]
        pairs, rest = crecv[slot, PRIMARY.index(k), 0:8], crecv[slot, PRIMARY.index(k), 8:16]
        for j in range(4):
            rows = pl.ds(32 * n + 8 * j, 8)
            mixed = jnp.where(lane_s >= 6, pltpu.roll(pairs, (6 - 2 * j) % SIZE, 1), recv[slot, axis, rows])
            recv[slot, axis, rows] = jnp.where((lane_s == 5) & (lane_i >= 12), pltpu.roll(rest, (5 - j) % SIZE, 1), mixed)
        mine = halo_lane & (sub // 4 == n)
        recv[slot, axis, 64:72] = jnp.where(mine, rest, recv[slot, axis, 64:72])

    def unpack_strip(arrs, axis, slot):
        for n, k in enumerate(STRIPS[axis]):
            for i in range(TILES):
                arrs[k, 8 * i + 6:8 * i + 8] = recv[slot, axis, 32 * n + 2 * i:32 * n + 2 * i + 2]
            for i in range(12, TILES):
                arrs[k, 8 * i + 5:8 * i + 6] = recv[slot, axis, 52 + 4 * n + i:53 + 4 * n + i]

    def own_rows(i):
        return sub < (6 if i < 12 else 5)

    def lanes_from(arrs, k, source):
        turned = tiles_of(source.T)
        for i in range(TILES):
            mask = halo_lane & own_rows(i) if k in PRIMARY else halo_lane
            arrs[k, 8 * i:8 * i + 8] = jnp.where(mask, turned[i], arrs[k, 8 * i:8 * i + 8])

    def ghosts(arrs):
        for k in range(6):
            near = ACROSS[k]
            arrs[k, 0:1] = arrs[near, 24:25]
            arrs[k, 8:9] = arrs[near, 16:17]

    def early_rows(arrs, out, slot):
        strip_copy(0, out, slot).wait()
        corner_copy(2, out, slot).wait()
        merge_corner(2, slot)
        corner_copy(4, out, slot).wait()
        merge_corner(4, slot)
        unpack_strip(arrs, 0, slot)
        strip_copy(1, out, slot).wait()
        corner_copy(0, out, slot).wait()
        merge_corner(0, slot)
        unpack_strip(arrs, 1, slot)

    def late_rows(arrs, out, slot):
        strip_copy(2, out, slot).wait()
        for n, k in enumerate(STRIPS[2]):
            for i in range(TILES):
                rows = pl.ds(8 * i + 6, 2)
                arrs[k, rows] = jnp.where(halo_lane[0:2], arrs[k, rows], recv[slot, 2, 32 * n + 2 * i:32 * n + 2 * i + 2])
            for i in range(12, TILES):
                rows = pl.ds(8 * i + 5, 1)
                arrs[k, rows] = jnp.where(halo_lane[0:1], arrs[k, rows], recv[slot, 2, 52 + 4 * n + i:53 + 4 * n + i])

    def scale_faces(first_step):
        def one(step, carry):
            scale = ws_ref[lax.rem(first_step + step, steps)]
            sw[step] = scale * wf[...]
            return carry
        lax.fori_loop(0, BLOCK_STEPS, one, 0)

    for f in (1, 2, 0):
        for slot in range(3):
            ox, oy, oz, quad = homes[slot]

            @pl.when(leaves[slot])
            def _():
                tile_copy(f, slot, quad, at(ox, oy, oz)).wait_send()
        for quad in range(3):
            @pl.when(comes[quad])
            def _():
                tile_copy(f, 0, quad, holder[quad]).wait_recv()
        for quad in range(3):
            loc = dot(dot(place_rows(flip_a[quad]), tiles[f, quad]), place_cols(flip_b[quad]))
            plain, turned = PLAIN[quad], TWIN[PLAIN[quad]]
            if f == 0:
                qa[plain] = loc
                qa[turned] = loc.T
            elif f == 1:
                loc = jnp.where(flip_a[quad] == 1, -1.0, 1.0) * loc
                qb[plain] = loc
                sw[0, turned] = loc.T
            else:
                loc = jnp.where(flip_b[quad] == 1, -1.0, 1.0) * loc
                sw[0, plain] = loc
                qb[turned] = loc.T
        if f == 2:
            start_all(qb, 1, 2, -1.0, 1.0)
            start_all(sw.at[0], 2, 3, 1.0, -1.0)
    start_all(qa, 0, 0, 1.0, 1.0)

    coef[0] = gain_ref[...]
    coef[1] = 1.0 - 4.0 * gain_ref[...]
    coef[2] = 0.5 * gain_ref[...]
    coef[3] = 0.5 - 2.0 * gain_ref[...]

    early_rows(qb, 1, 2)
    late_rows(qb, 1, 2)
    early_rows(sw.at[0], 2, 3)
    late_rows(sw.at[0], 2, 3)
    for k in range(6):
        lanes_from(qb, k, sw[0, TWIN[k]])
    for k in range(6):
        qb[k, 8:9] = -qb[ACROSS[k], 16:17]
    for k in range(6):
        here = qb[k]
        after = jnp.concatenate([here[8:], roll_rows(here[:8], -1)], axis=0)
        wf[k] = (0.5 / (6.0 * C_SPEED)) * (here + after)
    scale_faces(0)

    def lanes_and_ghosts(out, slot):
        for k in (1, 3, 4, 5):
            lanes_from(qa, k, qa[TWIN[k]])
        late_rows(qa, out, slot)
        for k in (0, 2):
            lanes_from(qa, k, qa[TWIN[k]])
        ghosts(qa)

    early_rows(qa, 0, 0)
    lanes_and_ghosts(0, 0)

    def x_part(a_ref, k, faces):
        a = a_ref[k]
        before = jnp.concatenate([a_ref[k, 119:127], a[:120]], axis=0)
        after = jnp.concatenate([a[8:], a_ref[k, 1:9]], axis=0)
        m = before + after
        v = 8.0 * a - m
        v_after = jnp.concatenate([v[8:], roll_rows(v[:8], -1)], axis=0)
        flux = faces * (v + v_after)
        flux_before = jnp.concatenate([roll_rows(flux[120:], 1), flux[:120]], axis=0)
        return (m - flux) + flux_before

    def stage(src, dst, second, step):
        ready = []
        for k in PRIMARY:
            t = TWIN[k]
            gain = coef[2 if second else 0]
            zk = gain * x_part(src, k, sw[step, k])
            own_part = coef[3 if second else 1] * src[k]
            if second:
                own_part = 0.5 * dst[k] + own_part
            zk = own_part + zk
            zt = gain * x_part(src, t, sw[step, t])
            ready.append((zk, zt))
        new = [None] * 6
        for k, (zk, zt) in zip(PRIMARY, ready):
            new[k] = zk + zt.T
            new[TWIN[k]] = zt + zk.T
        for k in range(6):
            dst[k] = new[k]
        for k in range(6):
            near = new[ACROSS[k]]
            dst[k, 0:1] = near[24:25]
            dst[k, 8:9] = near[16:17]

    def one_step(step, carry):
        stage(qa, qb, False, step)
        stage(qb, qa, True, step)
        return carry

    def run_steps(count):
        lax.fori_loop(0, count, one_step, 0, unroll=True)

    full_blocks = (steps - 1) // BLOCK_STEPS

    def block(blk, carry):
        run_steps(BLOCK_STEPS)
        slot = lax.rem(blk + 1, 2)
        start_all(qa, 0, slot, 1.0, 1.0)
        scale_faces((blk + 1) * BLOCK_STEPS)
        early_rows(qa, 0, slot)
        lanes_and_ghosts(0, slot)
        return carry

    lax.fori_loop(0, full_blocks, block, 0)
    run_steps(steps - full_blocks * BLOCK_STEPS)

    def result_copy(quad, slot, device, number):
        return pltpu.make_async_remote_copy(
            result.at[quad], out_ref.at[slot], osend.at[number], orecv.at[slot],
            device_id=device, device_id_type=MESH)

    for quad in range(3):
        result[quad] = dot(dot(place_cols(flip_a[quad]), qa[PLAIN[quad]]), place_rows(flip_b[quad]))

        @pl.when(comes[quad])
        def _():
            result_copy(quad, slot_of[quad], holder[quad], quad).start()

        @pl.when(jnp.logical_not(comes[quad]))
        def _():
            out_ref[slot_of[quad]] = result[quad]

    for quad in range(3):
        @pl.when(comes[quad])
        def _():
            result_copy(quad, slot_of[quad], holder[quad], quad).wait_send()
    for slot in range(3):
        ox, oy, oz, _ = homes[slot]

        @pl.when(leaves[slot])
        def _():
            result_copy(0, slot, at(ox, oy, oz), 0).wait_recv()
```

time: 238 us -> 210 us (0.88)
  Pallas kernels: 236 us -> 209 us
    pallas_call x1, Pallas kernels: 236 us -> 209 us  [local_run(): pl.pallas_call(functools.partial(kernel, own, steps, axis_names), out_sha...]
where the time goes in v2:
time: 210 us
  Pallas kernels  209 us (100%)
    pallas_call x1, Pallas kernels, local_run(): pl.pallas_call(functools.partial(kernel, own, steps, axis_names), out_sha...  209 us

profile of v2, /device:TPU:0, one launch (start us, length us, event | category | flops | bytes accessed | tf_op | source)
XLA Modules:
  0.0 210.3 jit_solution(18203079640399613208)
XLA Ops:
  0.0 208.7 %advect.1 = f32[3,90,90]{2,1,0:T(8,128)} custom-call(f32[256]{0:T(256)} %ws_ref.1, f32[3,90,90]{2,1,0:T(8,128)} %q_in.1, f32[3,90,90]{2,1,0:T(8,128)} %wa_in.1, f32[3,90,90]{2,1,0:T(8,128)} %wb_in.1, f32[128,128]{1,0:T(8,128)} %constant.2.clone.gain_ref), custom_call_target="tpu_custom_call" | custom-call | tf_op jit(solution)/shard_map/advect/pallas_call | solution.py:59
  208.7 1.6 copy.7

commit v3 on v2

--- a/solution.py
+++ b/solution.py
@@ -25,10 +25,22 @@
 LOW = 2
 OWN = 90
 BLOCK_STEPS = 9
-
-
-def pos_idx(pos):
-    return TILES * (pos % 8) + pos // 8
+LANE_ORDER = (8, 7, 9, 6, 10, 5, 11, 4, 12, 3, 13, 2, 14, 1, 15, 0)
+GROUPS = ((0, 2), (1, 3), (4, 5))
+
+
+def row_idx(row):
+    return TILES * (row % 8) + row // 8
+
+
+def lane_group(b):
+    half = (b + 1) // 2
+    return 8 - half + 2 * half * (1 - b % 2)
+
+
+def turn(arr):
+    turned = jnp.concatenate([arr[8 * i:8 * i + 8] for i in LANE_ORDER], axis=0).T
+    return jnp.concatenate([turned[8 * b:8 * b + 8] for b in map(LANE_ORDER.index, range(TILES))], axis=0)
 
 
 def tiles_of(arr):
@@ -51,8 +63,10 @@
         cells = 2 * own
         steps = wind_scale.shape[0]
         dalpha = 0.5 * math.pi / cells
-        tan_u = np.tan((pos_idx(np.arange(SIZE)) - LOW + 0.5) * dalpha - 0.25 * math.pi)
-        tan_a, tan_b = tan_u[:, None], tan_u[None, :]
+        place = np.arange(SIZE)
+        lane_idx = TILES * (place % 8) + lane_group(place // 8)
+        tan_a = np.tan((row_idx(place) - LOW + 0.5) * dalpha - 0.25 * math.pi)[:, None]
+        tan_b = np.tan((lane_idx - LOW + 0.5) * dalpha - 0.25 * math.pi)[None, :]
         r_sq = 1.0 + tan_a * tan_a + tan_b * tan_b
         inv_sqrt_g = r_sq * np.sqrt(r_sq) / ((1.0 + tan_a * tan_a) * (1.0 + tan_b * tan_b))
         gain = (0.5 * C_SPEED * CFL_STEP * inv_sqrt_g).astype(np.float32)
@@ -137,21 +151,20 @@
             def _():
                 tiles[f, quad] = fields[f][slot]
 
-    pos_r = lax.broadcasted_iota(jnp.int32, (SIZE, own), 0)
-    cell_c = lax.broadcasted_iota(jnp.int32, (SIZE, own), 1)
-    cell_r = lax.broadcasted_iota(jnp.int32, (own, SIZE), 0)
-    pos_c = lax.broadcasted_iota(jnp.int32, (own, SIZE), 1)
-
-    def spot(pos, flip):
-        dist = TILES * lax.rem(pos, 8) + pos // 8 - LOW
+    def placing(shape, spot_axis, to_idx, flip):
+        dist = to_idx(lax.broadcasted_iota(jnp.int32, shape, spot_axis)) - LOW
+        cell = lax.broadcasted_iota(jnp.int32, shape, 1 - spot_axis)
         inside = (dist >= 0) & (dist < own)
-        return jnp.where(inside, jnp.where(flip == 1, own - 1 - dist, dist), -1)
-
-    def place_rows(flip):
-        return jnp.where(spot(pos_r, flip) == cell_c, 1.0, 0.0)
-
-    def place_cols(flip):
-        return jnp.where(spot(pos_c, flip) == cell_r, 1.0, 0.0)
+        source = jnp.where(inside, jnp.where(flip == 1, own - 1 - dist, dist), -1)
+        return jnp.where(source == cell, 1.0, 0.0)
+
+    def row_to_idx(row):
+        return TILES * lax.rem(row, 8) + row // 8
+
+    def lane_to_idx(spot):
+        b = spot // 8
+        half = (b + 1) // 2
+        return TILES * lax.rem(spot, 8) + 8 - half + 2 * half * (1 - lax.rem(b, 2))
 
     def dot(lhs, rhs):
         return jnp.dot(lhs, rhs, precision=HIGHEST, preferred_element_type=jnp.float32)
@@ -160,12 +173,15 @@
 
     sub = lax.broadcasted_iota(jnp.int32, (8, SIZE), 0)
     lane = lax.broadcasted_iota(jnp.int32, (8, SIZE), 1)
-    lane_s, lane_i = lax.rem(lane, 8), lane // 8
+    lane_s, lane_i = lax.rem(lane, 8), lax.rem(lane_to_idx(lane), TILES)
     halo_lane = (lane_s >= 6) | ((lane_s == 5) & (lane_i >= 12))
-    mirror = jnp.where(lane_i < 8, 67, 194)
-    pair_src = mirror - (8 * lane_i + 6 + lax.rem(lane, 2))
-    edge_src = jnp.where(lane_i >= 12, 189 - 8 * lane_i, 0)
-    halo_src = jnp.where(halo_lane, mirror - lane, 0)
+
+    def mirror_lane(number):
+        return jnp.where(lane_i < 8, 8 * (1 + 2 * lane_i) + 11 - number, 8 * (30 - 2 * lane_i) + 10 - number)
+
+    pair_src = mirror_lane(6 + lax.rem(lane, 2))
+    edge_src = jnp.where(lane_i >= 12, mirror_lane(5), 0)
+    halo_src = jnp.where(halo_lane, mirror_lane(lane_s), 0)
     row_even, row_odd = 5 - lax.rem(sub, 2), 4 - lax.rem(sub, 2)
     row_pair, lane_pair = sub // 2, lane_s // 2
 
@@ -192,97 +208,98 @@
             csend.at[out, n], crecv.at[slot, n], ssem.at[slot, 3 + n], rsem.at[slot, 3 + n],
             device_id=peer(CORNERS[k][0]), device_id_type=MESH)
 
-    def pack_strip(get, axis, out, sign):
-        for n, k in enumerate(STRIPS[axis]):
-            a = [get(k, i) for i in range(TILES)]
+    def signed(sign, arr):
+        return arr if sign == 1.0 else sign * arr
+
+    def pack_strip(arrs, axis, out, sign):
+        msgs, tails = [], []
+        for k in STRIPS[axis]:
+            a = tiles_of(arrs[k])
             for j in range(4):
                 first, perm = (7, row_even) if j < 2 else (23, row_odd)
-                part = by_number(row_pair, [take(a[first - 4 * j - m], perm, 0) for m in range(4)])
-                send[out, axis, 32 * n + 8 * j:32 * n + 8 * j + 8] = sign * part if sign != 1.0 else part
-            tail = by_number(lax.rem(sub, 4), [take(a[11 - m], row_even * 0 + 5, 0) for m in range(4)])
-            tail = sign * tail if sign != 1.0 else tail
-            send[out, axis, 64 + 4 * n:68 + 4 * n] = tail[4 * n:4 * n + 4]
-
-    def pack_corner(k, out, sign):
-        _, axis, n = CORNERS[k]
-        msg = [send[out, axis, 32 * n + 8 * j:32 * n + 8 * j + 8] for j in range(4)]
-        tail = send[out, axis, 64:72]
+                msgs.append(signed(sign, by_number(row_pair, [take(a[first - 4 * j - m], perm, 0) for m in range(4)])))
+            tails.append(by_number(lax.rem(sub, 4), [take(a[11 - m], 0 * sub + 5, 0) for m in range(4)]))
+        tail = signed(sign, jnp.where(sub < 4, tails[0], tails[1]))
+        send[out, axis] = jnp.concatenate(msgs + [tail], axis=0)
+        return msgs, tail
+
+    def pack_corner(k, packed, out, sign):
+        n = CORNERS[k][2]
+        msg, tail = packed[0][4 * n:4 * n + 4], packed[1]
         pairs = by_number(lane_pair, [take(m, pair_src, 1) for m in msg])
         edges = by_number(lane_s, [take(m, edge_src, 1) for m in msg])
         rest = jnp.where(halo_lane, take(tail, halo_src, 1), edges)
-        slot = PRIMARY.index(k)
-        csend[out, slot, 0:8] = sign * pairs if sign != 1.0 else pairs
-        csend[out, slot, 8:16] = sign * rest if sign != 1.0 else rest
+        csend[out, PRIMARY.index(k)] = signed(sign, jnp.concatenate([pairs, rest], axis=0))
 
     def start_all(arrs, out, slot, row_sign, corner_sign):
-        def get(k, i):
-            return arrs[k, 8 * i:8 * i + 8]
-        pack_strip(get, 2, out, row_sign)
+        pack_strip(arrs, 2, out, row_sign)
         strip_copy(2, out, slot).start()
-        pack_strip(get, 1, out, row_sign)
-        pack_corner(0, out, corner_sign)
+        packed = [pack_strip(arrs, axis, out, row_sign) for axis in (0, 1)]
+        for k in PRIMARY:
+            pack_corner(k, packed[CORNERS[k][1]], out, corner_sign)
         corner_copy(0, out, slot).start()
-        pack_strip(get, 0, out, row_sign)
-        pack_corner(4, out, corner_sign)
         corner_copy(4, out, slot).start()
         strip_copy(1, out, slot).start()
-        pack_corner(2, out, corner_sign)
         corner_copy(2, out, slot).start()
         strip_copy(0, out, slot).start()
 
-    def merge_corner(k, slot):
-        _, axis, n = CORNERS[k]
-        pairs, rest = crecv[slot, PRIMARY.index(k), 0:8], crecv[slot, PRIMARY.index(k), 8:16]
-        for j in range(4):
-            rows = pl.ds(32 * n + 8 * j, 8)
-            mixed = jnp.where(lane_s >= 6, pltpu.roll(pairs, (6 - 2 * j) % SIZE, 1), recv[slot, axis, rows])
-            recv[slot, axis, rows] = jnp.where((lane_s == 5) & (lane_i >= 12), pltpu.roll(rest, (5 - j) % SIZE, 1), mixed)
-        mine = halo_lane & (sub // 4 == n)
-        recv[slot, axis, 64:72] = jnp.where(mine, rest, recv[slot, axis, 64:72])
-
-    def unpack_strip(arrs, axis, slot):
-        for n, k in enumerate(STRIPS[axis]):
-            for i in range(TILES):
-                arrs[k, 8 * i + 6:8 * i + 8] = recv[slot, axis, 32 * n + 2 * i:32 * n + 2 * i + 2]
-            for i in range(12, TILES):
-                arrs[k, 8 * i + 5:8 * i + 6] = recv[slot, axis, 52 + 4 * n + i:53 + 4 * n + i]
+    def halo_tiles(k, axis, n, slot, with_corner):
+        msg = [recv[slot, axis, 32 * n + 8 * j:32 * n + 8 * j + 8] for j in range(4)]
+        tail = recv[slot, axis, 64:72]
+        if with_corner:
+            pairs, rest = crecv[slot, PRIMARY.index(k), 0:8], crecv[slot, PRIMARY.index(k), 8:16]
+            edge = (lane_s == 5) & (lane_i >= 12)
+            for j in range(4):
+                mixed = jnp.where(lane_s >= 6, pltpu.roll(pairs, (6 - 2 * j) % SIZE, 1), msg[j])
+                msg[j] = jnp.where(edge, pltpu.roll(rest, (5 - j) % SIZE, 1), mixed)
+            tail = jnp.where(halo_lane, rest, tail)
+        res = []
+        for i in range(TILES):
+            tile = roll_rows(msg[i // 4], 6 - 2 * (i % 4))
+            if i >= 12:
+                tile = jnp.where(sub == 5, roll_rows(tail, 17 - i - 4 * n), tile)
+            res.append(tile)
+        return res
 
     def own_rows(i):
         return sub < (6 if i < 12 else 5)
 
-    def lanes_from(arrs, k, source):
-        turned = tiles_of(source.T)
+    def wait_all(out, slot):
+        for axis in (0, 1, 2):
+            strip_copy(axis, out, slot).wait()
+        for k in PRIMARY:
+            corner_copy(k, out, slot).wait()
+
+    def all_halos(slot):
+        halos = [None] * 6
+        for with_corner in (False, True):
+            for axis in range(3):
+                for n, k in enumerate(STRIPS[axis]):
+                    if (k in PRIMARY) == with_corner:
+                        halos[k] = halo_tiles(k, axis, n, slot, with_corner)
+        return halos
+
+    def merge(arrs, k, halos, lanes):
+        a, side = tiles_of(arrs[k]), tiles_of(lanes)
         for i in range(TILES):
-            mask = halo_lane & own_rows(i) if k in PRIMARY else halo_lane
-            arrs[k, 8 * i:8 * i + 8] = jnp.where(mask, turned[i], arrs[k, 8 * i:8 * i + 8])
-
-    def ghosts(arrs):
+            if k in PRIMARY:
+                new = jnp.where(own_rows(i), jnp.where(halo_lane, side[i], a[i]), halos[k][i])
+            else:
+                new = jnp.where(halo_lane, side[i], jnp.where(own_rows(i), a[i], halos[k][i]))
+            arrs[k, 8 * i:8 * i + 8] = new
+
+    def finish(slot):
+        wait_all(0, slot)
+        halos = all_halos(slot)
+        lanes = [None] * 6
+        for k in (1, 3, 5, 0, 2, 4):
+            lanes[TWIN[k]] = turn(join(halos[k]))
+        for k in (0, 2, 4, 1, 3, 5):
+            merge(qa, k, halos, lanes[k])
         for k in range(6):
             near = ACROSS[k]
-            arrs[k, 0:1] = arrs[near, 24:25]
-            arrs[k, 8:9] = arrs[near, 16:17]
-
-    def early_rows(arrs, out, slot):
-        strip_copy(0, out, slot).wait()
-        corner_copy(2, out, slot).wait()
-        merge_corner(2, slot)
-        corner_copy(4, out, slot).wait()
-        merge_corner(4, slot)
-        unpack_strip(arrs, 0, slot)
-        strip_copy(1, out, slot).wait()
-        corner_copy(0, out, slot).wait()
-        merge_corner(0, slot)
-        unpack_strip(arrs, 1, slot)
-
-    def late_rows(arrs, out, slot):
-        strip_copy(2, out, slot).wait()
-        for n, k in enumerate(STRIPS[2]):
-            for i in range(TILES):
-                rows = pl.ds(8 * i + 6, 2)
-                arrs[k, rows] = jnp.where(halo_lane[0:2], arrs[k, rows], recv[slot, 2, 32 * n + 2 * i:32 * n + 2 * i + 2])
-            for i in range(12, TILES):
-                rows = pl.ds(8 * i + 5, 1)
-                arrs[k, rows] = jnp.where(halo_lane[0:1], arrs[k, rows], recv[slot, 2, 52 + 4 * n + i:53 + 4 * n + i])
+            qa[k, 0:1] = qa[near, 24:25]
+            qa[k, 8:9] = qa[near, 16:17]
 
     def scale_faces(first_step):
         def one(step, carry):
@@ -303,19 +320,20 @@
             def _():
                 tile_copy(f, 0, quad, holder[quad]).wait_recv()
         for quad in range(3):
-            loc = dot(dot(place_rows(flip_a[quad]), tiles[f, quad]), place_cols(flip_b[quad]))
+            loc = dot(dot(placing((SIZE, own), 0, row_to_idx, flip_a[quad]), tiles[f, quad]),
+                      placing((own, SIZE), 1, lane_to_idx, flip_b[quad]))
             plain, turned = PLAIN[quad], TWIN[PLAIN[quad]]
             if f == 0:
                 qa[plain] = loc
-                qa[turned] = loc.T
+                qa[turned] = turn(loc)
             elif f == 1:
                 loc = jnp.where(flip_a[quad] == 1, -1.0, 1.0) * loc
                 qb[plain] = loc
-                sw[0, turned] = loc.T
+                sw[0, turned] = turn(loc)
             else:
                 loc = jnp.where(flip_b[quad] == 1, -1.0, 1.0) * loc
                 sw[0, plain] = loc
-                qb[turned] = loc.T
+                qb[turned] = turn(loc)
         if f == 2:
             start_all(qb, 1, 2, -1.0, 1.0)
             start_all(sw.at[0], 2, 3, 1.0, -1.0)
@@ -326,12 +344,11 @@
     coef[2] = 0.5 * gain_ref[...]
     coef[3] = 0.5 - 2.0 * gain_ref[...]
 
-    early_rows(qb, 1, 2)
-    late_rows(qb, 1, 2)
-    early_rows(sw.at[0], 2, 3)
-    late_rows(sw.at[0], 2, 3)
+    wait_all(1, 2)
+    wait_all(2, 3)
+    wind_halos, side_halos = all_halos(2), all_halos(3)
     for k in range(6):
-        lanes_from(qb, k, sw[0, TWIN[k]])
+        merge(qb, k, wind_halos, turn(join(side_halos[TWIN[k]])))
     for k in range(6):
         qb[k, 8:9] = -qb[ACROSS[k], 16:17]
     for k in range(6):
@@ -339,17 +356,6 @@
         after = jnp.concatenate([here[8:], roll_rows(here[:8], -1)], axis=0)
         wf[k] = (0.5 / (6.0 * C_SPEED)) * (here + after)
     scale_faces(0)
-
-    def lanes_and_ghosts(out, slot):
-        for k in (1, 3, 4, 5):
-            lanes_from(qa, k, qa[TWIN[k]])
-        late_rows(qa, out, slot)
-        for k in (0, 2):
-            lanes_from(qa, k, qa[TWIN[k]])
-        ghosts(qa)
-
-    early_rows(qa, 0, 0)
-    lanes_and_ghosts(0, 0)
 
     def x_part(a_ref, k, faces):
         a = a_ref[k]
@@ -363,21 +369,18 @@
         return (m - flux) + flux_before
 
     def stage(src, dst, second, step):
-        ready = []
-        for k in PRIMARY:
-            t = TWIN[k]
-            gain = coef[2 if second else 0]
-            zk = gain * x_part(src, k, sw[step, k])
-            own_part = coef[3 if second else 1] * src[k]
-            if second:
-                own_part = 0.5 * dst[k] + own_part
-            zk = own_part + zk
-            zt = gain * x_part(src, t, sw[step, t])
-            ready.append((zk, zt))
-        new = [None] * 6
-        for k, (zk, zt) in zip(PRIMARY, ready):
-            new[k] = zk + zt.T
-            new[TWIN[k]] = zt + zk.T
+        part, turned = [None] * 6, [None] * 6
+        for group in GROUPS:
+            for k in group:
+                part[k] = coef[2 if second else 0] * x_part(src, k, sw[step, k])
+                if k in PRIMARY:
+                    own_part = coef[3 if second else 1] * src[k]
+                    if second:
+                        own_part = 0.5 * dst[k] + own_part
+                    part[k] = own_part + part[k]
+            for k in group:
+                turned[k] = turn(part[k])
+        new = [part[k] + turned[TWIN[k]] for k in range(6)]
         for k in range(6):
             dst[k] = new[k]
         for k in range(6):
@@ -396,15 +399,14 @@
     full_blocks = (steps - 1) // BLOCK_STEPS
 
     def block(blk, carry):
+        finish(lax.rem(blk, 2))
         run_steps(BLOCK_STEPS)
-        slot = lax.rem(blk + 1, 2)
-        start_all(qa, 0, slot, 1.0, 1.0)
+        start_all(qa, 0, lax.rem(blk + 1, 2), 1.0, 1.0)
         scale_faces((blk + 1) * BLOCK_STEPS)
-        early_rows(qa, 0, slot)
-        lanes_and_ghosts(0, slot)
         return carry
 
     lax.fori_loop(0, full_blocks, block, 0)
+    finish(full_blocks % 2)
     run_steps(steps - full_blocks * BLOCK_STEPS)
 
     def result_copy(quad, slot, device, number):
@@ -413,7 +415,8 @@
             device_id=device, device_id_type=MESH)
 
     for quad in range(3):
-        result[quad] = dot(dot(place_cols(flip_a[quad]), qa[PLAIN[quad]]), place_rows(flip_b[quad]))
+        result[quad] = dot(dot(placing((own, SIZE), 1, row_to_idx, flip_a[quad]), qa[PLAIN[quad]]),
+                           placing((SIZE, own), 0, lane_to_idx, flip_b[quad]))
 
         @pl.when(comes[quad])
         def _():

time: 210 us -> 190 us (0.905)
  Pallas kernels: 209 us -> 188 us
    pallas_call x1, Pallas kernels: 209 us -> 188 us  [local_run(): pl.pallas_call(functools.partial(kernel, own, steps, axis_names), out_sha...]
where the time goes in v3:
time: 190 us
  Pallas kernels  188 us (99%)
    pallas_call x1, Pallas kernels, local_run(): pl.pallas_call(functools.partial(kernel, own, steps, axis_names), out_sha...  188 us

profile of v3, /device:TPU:0, one launch (start us, length us, event | category | flops | bytes accessed | tf_op | source)
XLA Modules:
  0.0 190.0 jit_solution(3228693866169527164)
XLA Ops:
  0.0 188.4 %advect.1 = f32[3,90,90]{2,1,0:T(8,128)} custom-call(f32[256]{0:T(256)} %ws_ref.1, f32[3,90,90]{2,1,0:T(8,128)} %q_in.1, f32[3,90,90]{2,1,0:T(8,128)} %wa_in.1, f32[3,90,90]{2,1,0:T(8,128)} %wb_in.1, f32[128,128]{1,0:T(8,128)} %constant.2.clone.gain_ref), custom_call_target="tpu_custom_call" | custom-call | tf_op jit(solution)/shard_map/advect/pallas_call | solution.py:73
  188.4 1.6 copy.7

commit v4 on v3

--- a/solution.py
+++ b/solution.py
@@ -18,7 +18,8 @@
 ACROSS = (2, 4, 0, 5, 1, 3)
 PRIMARY = (0, 2, 4)
 STRIPS = ((2, 4), (0, 5), (1, 3))
-CORNERS = {0: ((0, 1, 1), 1, 0), 2: ((1, 0, 1), 0, 0), 4: ((1, 1, 0), 0, 1)}
+STRIP_PLACE = {k: (axis, n) for axis in range(3) for n, k in enumerate(STRIPS[axis])}
+CORNERS = {0: (0, 1, 1), 2: (1, 0, 1), 4: (1, 1, 0)}
 
 SIZE = 128
 TILES = 16
@@ -73,9 +74,11 @@
         out = pl.pallas_call(
             functools.partial(kernel, own, steps, axis_names),
             out_shape=jax.ShapeDtypeStruct(tracer.shape, jnp.float32),
-            in_specs=[pl.BlockSpec(memory_space=pltpu.SMEM)] + [pl.BlockSpec(memory_space=pltpu.VMEM)] * 4,
-            out_specs=pl.BlockSpec(memory_space=pltpu.VMEM),
+            in_specs=[pl.BlockSpec(memory_space=pl.ANY)] * 5,
+            out_specs=pl.BlockSpec(memory_space=pl.ANY),
             scratch_shapes=[
+                pltpu.SMEM((steps,), jnp.float32),
+                pltpu.VMEM((3, 3, own, own), jnp.float32),
                 pltpu.VMEM((6, SIZE, SIZE), jnp.float32),
                 pltpu.VMEM((6, SIZE, SIZE), jnp.float32),
                 pltpu.VMEM((BLOCK_STEPS, 6, SIZE, SIZE), jnp.float32),
@@ -93,7 +96,9 @@
                 pltpu.SemaphoreType.DMA((3, 3)),
                 pltpu.SemaphoreType.DMA((3,)),
                 pltpu.SemaphoreType.DMA((3,)),
+                pltpu.SemaphoreType.DMA((5,)),
             ],
+            compiler_params=pltpu.CompilerParams(collective_id=0, has_side_effects=True),
             name="advect",
         )(wind_scale, tracer, wind_a, wind_b, gain)
         return out
@@ -104,14 +109,23 @@
                          out_specs=field_spec, check_vma=False)
 
 
-def kernel(own, steps, axis_names, ws_ref, q_in, wa_in, wb_in, gain_ref, out_ref,
-           qa, qb, sw, wf, coef, tiles, result, send, recv, csend, crecv,
-           ssem, rsem, tsend, trecv, osend, orecv):
+def kernel(own, steps, axis_names, ws_in, q_in, wa_in, wb_in, gain_in, out_ref,
+           ws_ref, fields, qa, qb, sw, wf, coef, tiles, result, send, recv, csend, crecv,
+           ssem, rsem, tsend, trecv, osend, orecv, isem):
     tx, ty, core = lax.axis_index('tx'), lax.axis_index('ty'), lax.axis_index('panel')
     by, bz, bx = tx, ty, lax.rem(core + tx + 1, 2)
 
     def place(kx, ky, kc):
         return {name: {'tx': kx, 'ty': ky, 'panel': kc}.get(name, 0) for name in axis_names}
+
+    barrier = pltpu.get_barrier_semaphore()
+    for other in range(1, 8):
+        near = [1 - at if other & bit else at for at, bit in ((tx, 1), (ty, 2), (core, 4))]
+        pl.semaphore_signal(barrier, inc=1, device_id=place(*near), device_id_type=MESH)
+    loads = [pltpu.make_async_copy(src, dst, isem.at[n]) for n, (src, dst) in enumerate((
+        (wa_in, fields.at[1]), (wb_in, fields.at[2]), (q_in, fields.at[0]), (gain_in, coef.at[0]), (ws_in, ws_ref)))]
+    for load in loads:
+        load.start()
 
     def at(ox, oy, oz):
         return place(oy, oz, lax.rem(ox + oy + 1, 2))
@@ -132,13 +146,14 @@
     slot_of = [lax.rem(panel[n], 3) for n in range(3)]
     comes = [jnp.logical_not((flip_a[n] == tx) & (flip_b[n] == ty) & (panel[n] // 3 == core)) for n in range(3)]
 
-    fields = (q_in, wa_in, wb_in)
-
     def tile_copy(f, slot, quad, device):
         return pltpu.make_async_remote_copy(
-            fields[f].at[slot], tiles.at[f, quad], tsend.at[f, slot], trecv.at[f, quad],
+            fields.at[f, slot], tiles.at[f, quad], tsend.at[f, slot], trecv.at[f, quad],
             device_id=device, device_id_type=MESH)
 
+    for load in loads:
+        load.wait()
+    pl.semaphore_wait(barrier, 7)
     for f in (1, 2, 0):
         for slot in range(3):
             ox, oy, oz, quad = homes[slot]
@@ -149,7 +164,7 @@
 
             @pl.when(jnp.logical_not(leaves[slot]))
             def _():
-                tiles[f, quad] = fields[f][slot]
+                tiles[f, quad] = fields[f, slot]
 
     def placing(shape, spot_axis, to_idx, flip):
         dist = to_idx(lax.broadcasted_iota(jnp.int32, shape, spot_axis)) - LOW
@@ -206,41 +221,41 @@
         n = PRIMARY.index(k)
         return pltpu.make_async_remote_copy(
             csend.at[out, n], crecv.at[slot, n], ssem.at[slot, 3 + n], rsem.at[slot, 3 + n],
-            device_id=peer(CORNERS[k][0]), device_id_type=MESH)
+            device_id=peer(CORNERS[k]), device_id_type=MESH)
 
     def signed(sign, arr):
         return arr if sign == 1.0 else sign * arr
 
-    def pack_strip(arrs, axis, out, sign):
-        msgs, tails = [], []
-        for k in STRIPS[axis]:
-            a = tiles_of(arrs[k])
-            for j in range(4):
-                first, perm = (7, row_even) if j < 2 else (23, row_odd)
-                msgs.append(signed(sign, by_number(row_pair, [take(a[first - 4 * j - m], perm, 0) for m in range(4)])))
-            tails.append(by_number(lax.rem(sub, 4), [take(a[11 - m], 0 * sub + 5, 0) for m in range(4)]))
-        tail = signed(sign, jnp.where(sub < 4, tails[0], tails[1]))
-        send[out, axis] = jnp.concatenate(msgs + [tail], axis=0)
-        return msgs, tail
-
-    def pack_corner(k, packed, out, sign):
-        n = CORNERS[k][2]
-        msg, tail = packed[0][4 * n:4 * n + 4], packed[1]
-        pairs = by_number(lane_pair, [take(m, pair_src, 1) for m in msg])
-        edges = by_number(lane_s, [take(m, edge_src, 1) for m in msg])
-        rest = jnp.where(halo_lane, take(tail, halo_src, 1), edges)
-        csend[out, PRIMARY.index(k)] = signed(sign, jnp.concatenate([pairs, rest], axis=0))
-
-    def start_all(arrs, out, slot, row_sign, corner_sign):
-        pack_strip(arrs, 2, out, row_sign)
+    def pack(arrs, k, out, sign, corner_sign):
+        axis, n = STRIP_PLACE[k]
+        a = tiles_of(arrs[k])
+        msg = []
+        for j in range(4):
+            first, perm = (7, row_even) if j < 2 else (23, row_odd)
+            msg.append(signed(sign, by_number(row_pair, [take(a[first - 4 * j - m], perm, 0) for m in range(4)])))
+        tail = signed(sign, by_number(lax.rem(sub, 4), [take(a[11 - m], 0 * sub + 5, 0) for m in range(4)]))
+        send[out, axis, 32 * n:32 * n + 32] = jnp.concatenate(msg, axis=0)
+        send[out, axis, 64 + 4 * n:68 + 4 * n] = tail[4 * n:4 * n + 4]
+        if k in PRIMARY:
+            pairs = by_number(lane_pair, [take(m, pair_src, 1) for m in msg])
+            edges = by_number(lane_s, [take(m, edge_src, 1) for m in msg])
+            rest = jnp.where(halo_lane, take(tail, halo_src, 1), edges)
+            csend[out, PRIMARY.index(k)] = signed(corner_sign, jnp.concatenate([pairs, rest], axis=0))
+
+    def start_first(arrs, out, slot, sign, corner_sign):
+        for k in (1, 3):
+            pack(arrs, k, out, sign, corner_sign)
         strip_copy(2, out, slot).start()
-        packed = [pack_strip(arrs, axis, out, row_sign) for axis in (0, 1)]
-        for k in PRIMARY:
-            pack_corner(k, packed[CORNERS[k][1]], out, corner_sign)
-        corner_copy(0, out, slot).start()
+        for k in (0, 2):
+            pack(arrs, k, out, sign, corner_sign)
+        for k in (0, 2):
+            corner_copy(k, out, slot).start()
+
+    def start_rest(arrs, out, slot, sign, corner_sign):
+        for k in (4, 5):
+            pack(arrs, k, out, sign, corner_sign)
         corner_copy(4, out, slot).start()
         strip_copy(1, out, slot).start()
-        corner_copy(2, out, slot).start()
         strip_copy(0, out, slot).start()
 
     def halo_tiles(k, axis, n, slot, with_corner):
@@ -265,37 +280,34 @@
         return sub < (6 if i < 12 else 5)
 
     def wait_all(out, slot):
-        for axis in (0, 1, 2):
+        for axis in (0, 1):
             strip_copy(axis, out, slot).wait()
-        for k in PRIMARY:
+        for k in (2, 4, 0):
             corner_copy(k, out, slot).wait()
-
-    def all_halos(slot):
-        halos = [None] * 6
-        for with_corner in (False, True):
-            for axis in range(3):
-                for n, k in enumerate(STRIPS[axis]):
-                    if (k in PRIMARY) == with_corner:
-                        halos[k] = halo_tiles(k, axis, n, slot, with_corner)
+        strip_copy(2, out, slot).wait()
+
+    def halos_of(slot):
+        halos = {}
+        for k in (1, 3, 5, 0, 2, 4):
+            halos[k] = halo_tiles(k, *STRIP_PLACE[k], slot, k in PRIMARY)
         return halos
 
-    def merge(arrs, k, halos, lanes):
-        a, side = tiles_of(arrs[k]), tiles_of(lanes)
+    def merge(arrs, k, rows, lanes):
+        side = tiles_of(lanes)
         for i in range(TILES):
+            new = arrs[k, 8 * i:8 * i + 8]
             if k in PRIMARY:
-                new = jnp.where(own_rows(i), jnp.where(halo_lane, side[i], a[i]), halos[k][i])
+                new = jnp.where(own_rows(i), jnp.where(halo_lane, side[i], new), rows[i])
             else:
-                new = jnp.where(halo_lane, side[i], jnp.where(own_rows(i), a[i], halos[k][i]))
+                new = jnp.where(halo_lane, side[i], jnp.where(own_rows(i), new, rows[i]))
             arrs[k, 8 * i:8 * i + 8] = new
 
     def finish(slot):
         wait_all(0, slot)
-        halos = all_halos(slot)
-        lanes = [None] * 6
-        for k in (1, 3, 5, 0, 2, 4):
-            lanes[TWIN[k]] = turn(join(halos[k]))
+        halos = halos_of(slot)
+        lanes = {TWIN[k]: turn(join(halos[k])) for k in (1, 3, 5, 0, 2, 4)}
         for k in (0, 2, 4, 1, 3, 5):
-            merge(qa, k, halos, lanes[k])
+            merge(qa, k, halos[k], lanes[k])
         for k in range(6):
             near = ACROSS[k]
             qa[k, 0:1] = qa[near, 24:25]
@@ -335,20 +347,22 @@
                 sw[0, plain] = loc
                 qb[turned] = turn(loc)
         if f == 2:
-            start_all(qb, 1, 2, -1.0, 1.0)
-            start_all(sw.at[0], 2, 3, 1.0, -1.0)
-    start_all(qa, 0, 0, 1.0, 1.0)
-
-    coef[0] = gain_ref[...]
-    coef[1] = 1.0 - 4.0 * gain_ref[...]
-    coef[2] = 0.5 * gain_ref[...]
-    coef[3] = 0.5 - 2.0 * gain_ref[...]
+            start_first(qb, 1, 2, -1.0, 1.0)
+            start_rest(qb, 1, 2, -1.0, 1.0)
+            start_first(sw.at[0], 2, 3, 1.0, -1.0)
+            start_rest(sw.at[0], 2, 3, 1.0, -1.0)
+    start_first(qa, 0, 0, 1.0, 1.0)
+    start_rest(qa, 0, 0, 1.0, 1.0)
+
+    coef[1] = 1.0 - 4.0 * coef[0]
+    coef[2] = 0.5 * coef[0]
+    coef[3] = 0.5 - 2.0 * coef[0]
 
     wait_all(1, 2)
     wait_all(2, 3)
-    wind_halos, side_halos = all_halos(2), all_halos(3)
+    wind_halos, side_halos = halos_of(2), halos_of(3)
     for k in range(6):
-        merge(qb, k, wind_halos, turn(join(side_halos[TWIN[k]])))
+        merge(qb, k, wind_halos[k], turn(join(side_halos[TWIN[k]])))
     for k in range(6):
         qb[k, 8:9] = -qb[ACROSS[k], 16:17]
     for k in range(6):
@@ -368,46 +382,60 @@
         flux_before = jnp.concatenate([roll_rows(flux[120:], 1), flux[:120]], axis=0)
         return (m - flux) + flux_before
 
-    def stage(src, dst, second, step):
-        part, turned = [None] * 6, [None] * 6
+    def parts_of(src, dst, second, step, group):
+        part = {}
+        for k in group:
+            part[k] = coef[2 if second else 0] * x_part(src, k, sw[step, k])
+            if k in PRIMARY:
+                own_part = coef[3 if second else 1] * src[k]
+                if second:
+                    own_part = 0.5 * dst[k] + own_part
+                part[k] = own_part + part[k]
+        return part, {k: turn(part[k]) for k in group}
+
+    def stage(src, dst, second, step, before_end=None):
+        part, turned = {}, {}
         for group in GROUPS:
-            for k in group:
-                part[k] = coef[2 if second else 0] * x_part(src, k, sw[step, k])
-                if k in PRIMARY:
-                    own_part = coef[3 if second else 1] * src[k]
-                    if second:
-                        own_part = 0.5 * dst[k] + own_part
-                    part[k] = own_part + part[k]
-            for k in group:
-                turned[k] = turn(part[k])
-        new = [part[k] + turned[TWIN[k]] for k in range(6)]
-        for k in range(6):
-            dst[k] = new[k]
-        for k in range(6):
-            near = new[ACROSS[k]]
-            dst[k, 0:1] = near[24:25]
-            dst[k, 8:9] = near[16:17]
-
-    def one_step(step, carry):
-        stage(qa, qb, False, step)
-        stage(qb, qa, True, step)
-        return carry
-
-    def run_steps(count):
-        lax.fori_loop(0, count, one_step, 0, unroll=True)
+            more = parts_of(src, dst, second, step, group)
+            part.update(more[0])
+            turned.update(more[1])
+        new = {}
+        for pair in ((0, 1, 2, 3), (4, 5)):
+            for k in pair:
+                new[k] = part[k] + turned[TWIN[k]]
+            for k in pair:
+                dst[k] = new[k]
+            if before_end is not None and pair == (0, 1, 2, 3):
+                before_end()
+        if before_end is None:
+            for k in range(6):
+                near = new[ACROSS[k]]
+                dst[k, 0:1] = near[24:25]
+                dst[k, 8:9] = near[16:17]
+
+    def run_block(count, slot, before_end):
+        finish(slot)
+
+        def one_step(step, carry):
+            stage(qa, qb, False, step)
+            stage(qb, qa, True, step)
+            return carry
+
+        lax.fori_loop(0, count - 1, one_step, 0, unroll=True)
+        stage(qa, qb, False, count - 1)
+        stage(qb, qa, True, count - 1, before_end=before_end)
 
     full_blocks = (steps - 1) // BLOCK_STEPS
 
     def block(blk, carry):
-        finish(lax.rem(blk, 2))
-        run_steps(BLOCK_STEPS)
-        start_all(qa, 0, lax.rem(blk + 1, 2), 1.0, 1.0)
+        out_slot = lax.rem(blk + 1, 2)
+        run_block(BLOCK_STEPS, lax.rem(blk, 2), functools.partial(start_first, qa, 0, out_slot, 1.0, 1.0))
+        start_rest(qa, 0, out_slot, 1.0, 1.0)
         scale_faces((blk + 1) * BLOCK_STEPS)
         return carry
 
     lax.fori_loop(0, full_blocks, block, 0)
-    finish(full_blocks % 2)
-    run_steps(steps - full_blocks * BLOCK_STEPS)
+    run_block(steps - full_blocks * BLOCK_STEPS, full_blocks % 2, lambda: None)
 
     def result_copy(quad, slot, device, number):
         return pltpu.make_async_remote_copy(
@@ -424,12 +452,16 @@
 
         @pl.when(jnp.logical_not(comes[quad]))
         def _():
-            out_ref[slot_of[quad]] = result[quad]
+            pltpu.make_async_copy(result.at[quad], out_ref.at[slot_of[quad]], osend.at[quad]).start()
 
     for quad in range(3):
         @pl.when(comes[quad])
         def _():
             result_copy(quad, slot_of[quad], holder[quad], quad).wait_send()
+
+        @pl.when(jnp.logical_not(comes[quad]))
+        def _():
+            pltpu.make_async_copy(result.at[quad], out_ref.at[slot_of[quad]], osend.at[quad]).wait()
     for slot in range(3):
         ox, oy, oz, _ = homes[slot]
 

time: 190 us -> 184 us (0.968)
  Pallas kernels: 188 us -> 182 us
    pallas_call x1, Pallas kernels: 188 us -> 182 us  [local_run(): pl.pallas_call(functools.partial(kernel, own, steps, axis_names), out_sha...]
where the time goes in v4:
time: 184 us
  Pallas kernels  182 us (99%)
    pallas_call x1, Pallas kernels, local_run(): pl.pallas_call(functools.partial(kernel, own, steps, axis_names), out_sha...  182 us

profile of v4, /device:TPU:0, one launch (start us, length us, event | category | flops | bytes accessed | tf_op | source)
XLA Modules:
  0.0 183.9 jit_solution(1092852353478801344)
XLA Ops:
  0.0 182.3 %advect.1 = f32[3,90,90]{2,1,0:T(8,128)} custom-call(f32[256]{0:T(256)} %ws_in.1, f32[3,90,90]{2,1,0:T(8,128)} %q_in.1, f32[3,90,90]{2,1,0:T(8,128)} %wa_in.1, f32[3,90,90]{2,1,0:T(8,128)} %wb_in.1, f32[128,128]{1,0:T(8,128)} %constant.2.clone.gain_in), custom_call_target="tpu_custom_call" | custom-call | tf_op jit(solution)/shard_map/advect/pallas_call | solution.py:74
  182.3 1.6 copy.7

commit v5 on v4

--- a/solution.py
+++ b/solution.py
@@ -39,21 +39,30 @@
     return 8 - half + 2 * half * (1 - b % 2)
 
 
-def turn(arr):
-    turned = jnp.concatenate([arr[8 * i:8 * i + 8] for i in LANE_ORDER], axis=0).T
-    return jnp.concatenate([turned[8 * b:8 * b + 8] for b in map(LANE_ORDER.index, range(TILES))], axis=0)
+def tile(i, offset=0):
+    return pl.ds(8 * i + offset, 8)
+
+
+def row(i, offset=0):
+    return pl.ds(8 * i + offset, 1)
 
 
 def tiles_of(arr):
-    return [arr[8 * i:8 * i + 8] for i in range(arr.shape[0] // 8)]
+    return jnp.split(arr, arr.shape[0] // 8)
 
 
 def join(tiles):
-    return jnp.concatenate(tiles, axis=0)
+    return jnp.concatenate(tiles)
 
 
 def roll_rows(tile, shift):
     return pltpu.roll(tile, shift % 8, 0)
+
+
+def turn(arr):
+    tiles = tiles_of(arr)
+    turned = tiles_of(join([tiles[i] for i in LANE_ORDER]).T)
+    return join([turned[LANE_ORDER.index(i)] for i in range(TILES)])
 
 
 def solution(mesh):
@@ -88,8 +97,8 @@
                 pltpu.VMEM((3, own, own), jnp.float32),
                 pltpu.VMEM((3, 3, 72, SIZE), jnp.float32),
                 pltpu.VMEM((4, 3, 72, SIZE), jnp.float32),
-                pltpu.VMEM((3, 3, 16, SIZE), jnp.float32),
-                pltpu.VMEM((4, 3, 16, SIZE), jnp.float32),
+                pltpu.VMEM((3, 3, 8, SIZE), jnp.float32),
+                pltpu.VMEM((4, 3, 8, SIZE), jnp.float32),
                 pltpu.SemaphoreType.DMA((4, 6)),
                 pltpu.SemaphoreType.DMA((4, 6)),
                 pltpu.SemaphoreType.DMA((3, 3)),
@@ -194,14 +203,23 @@
     def mirror_lane(number):
         return jnp.where(lane_i < 8, 8 * (1 + 2 * lane_i) + 11 - number, 8 * (30 - 2 * lane_i) + 10 - number)
 
-    pair_src = mirror_lane(6 + lax.rem(lane, 2))
-    edge_src = jnp.where(lane_i >= 12, mirror_lane(5), 0)
-    halo_src = jnp.where(halo_lane, mirror_lane(lane_s), 0)
-    row_even, row_odd = 5 - lax.rem(sub, 2), 4 - lax.rem(sub, 2)
+    odd_row, odd_lane = lax.rem(sub, 2), lax.rem(lane, 2)
+    pair_src = mirror_lane(6 + odd_lane)
     row_pair, lane_pair = sub // 2, lane_s // 2
-
-    def take(tile, idx, axis):
-        return jnp.take_along_axis(tile, idx, axis=axis, mode="promise_in_bounds")
+    late_group = lane_i >= 14
+    from_twin = (lane_pair == 2) | ((lane_pair == 3) & jnp.logical_not(late_group))
+    twin_src = jnp.where(from_twin, mirror_lane(4 + lane_pair), 0)
+    inner_src = jnp.where(lane_pair == 3, mirror_lane(5), 8 * (34 - 2 * lane_i) + 5)
+    primary_src = jnp.where(from_twin, 0, jnp.where((lane_pair > 0) & late_group, inner_src, mirror_lane(6 + lane_pair)))
+    inner_lane = jnp.where(late_group, 16 * lane_i - 121, 16 * lane_i - 93)
+    primary_back = jnp.where(lane_s == 6, lane - 5, jnp.where(lane_s == 7, lane - 4, jnp.where(halo_lane, inner_lane, 0)))
+    twin_back = jnp.where(lane_s == 6, lane - 1, lane)
+
+    def rows_by(arr, idx):
+        return jnp.take_along_axis(arr, idx, axis=0, mode="promise_in_bounds")
+
+    def lanes_by(arr, idx):
+        return jnp.take_along_axis(arr, idx, axis=1, mode="promise_in_bounds")
 
     def by_number(number, parts):
         res = parts[3]
@@ -226,58 +244,53 @@
     def signed(sign, arr):
         return arr if sign == 1.0 else sign * arr
 
-    def pack(arrs, k, out, sign, corner_sign):
+    def pack(arrs, k, out, sign):
         axis, n = STRIP_PLACE[k]
         a = tiles_of(arrs[k])
         msg = []
         for j in range(4):
-            first, perm = (7, row_even) if j < 2 else (23, row_odd)
-            msg.append(signed(sign, by_number(row_pair, [take(a[first - 4 * j - m], perm, 0) for m in range(4)])))
-        tail = signed(sign, by_number(lax.rem(sub, 4), [take(a[11 - m], 0 * sub + 5, 0) for m in range(4)]))
-        send[out, axis, 32 * n:32 * n + 32] = jnp.concatenate(msg, axis=0)
-        send[out, axis, 64 + 4 * n:68 + 4 * n] = tail[4 * n:4 * n + 4]
-        if k in PRIMARY:
-            pairs = by_number(lane_pair, [take(m, pair_src, 1) for m in msg])
-            edges = by_number(lane_s, [take(m, edge_src, 1) for m in msg])
-            rest = jnp.where(halo_lane, take(tail, halo_src, 1), edges)
-            csend[out, PRIMARY.index(k)] = signed(corner_sign, jnp.concatenate([pairs, rest], axis=0))
+            first, sublane = (7, 5 - odd_row) if j < 2 else (23, 4 - odd_row)
+            msg.append(signed(sign, by_number(row_pair, [rows_by(a[first - 4 * j - m], sublane) for m in range(4)])))
+        tail = signed(sign, by_number(lax.rem(sub, 4), [rows_by(a[11 - m], 5 + 0 * sub) for m in range(4)]))
+        send[out, axis, pl.ds(32 * n, 32)] = join(msg)
+        send[out, axis, pl.ds(64 + 4 * n, 4)] = tail[4 * n:4 * n + 4]
+        return msg, tail
+
+    def pack_pair(arrs, k, out, sign, corner_sign, twin_tail):
+        msg, tail = pack(arrs, k, out, sign)
+        pairs = by_number(lane_pair, [lanes_by(m, pair_src) for m in msg])
+        inner = jnp.where(from_twin, lanes_by(rows_by(twin_tail, row_pair), twin_src), lanes_by(rows_by(tail, row_pair), primary_src))
+        csend[out, PRIMARY.index(k)] = signed(corner_sign, jnp.where(odd_row * odd_lane == 1, inner, pairs))
 
     def start_first(arrs, out, slot, sign, corner_sign):
-        for k in (1, 3):
-            pack(arrs, k, out, sign, corner_sign)
+        tails = [pack(arrs, k, out, sign)[1] for k in (1, 3)]
         strip_copy(2, out, slot).start()
-        for k in (0, 2):
-            pack(arrs, k, out, sign, corner_sign)
+        for k, tail in zip((0, 2), tails):
+            pack_pair(arrs, k, out, sign, corner_sign, tail)
         for k in (0, 2):
             corner_copy(k, out, slot).start()
 
     def start_rest(arrs, out, slot, sign, corner_sign):
-        for k in (4, 5):
-            pack(arrs, k, out, sign, corner_sign)
+        pack_pair(arrs, 4, out, sign, corner_sign, pack(arrs, 5, out, sign)[1])
         corner_copy(4, out, slot).start()
         strip_copy(1, out, slot).start()
         strip_copy(0, out, slot).start()
 
-    def halo_tiles(k, axis, n, slot, with_corner):
-        msg = [recv[slot, axis, 32 * n + 8 * j:32 * n + 8 * j + 8] for j in range(4)]
-        tail = recv[slot, axis, 64:72]
-        if with_corner:
-            pairs, rest = crecv[slot, PRIMARY.index(k), 0:8], crecv[slot, PRIMARY.index(k), 8:16]
-            edge = (lane_s == 5) & (lane_i >= 12)
-            for j in range(4):
-                mixed = jnp.where(lane_s >= 6, pltpu.roll(pairs, (6 - 2 * j) % SIZE, 1), msg[j])
-                msg[j] = jnp.where(edge, pltpu.roll(rest, (5 - j) % SIZE, 1), mixed)
-            tail = jnp.where(halo_lane, rest, tail)
-        res = []
-        for i in range(TILES):
-            tile = roll_rows(msg[i // 4], 6 - 2 * (i % 4))
-            if i >= 12:
-                tile = jnp.where(sub == 5, roll_rows(tail, 17 - i - 4 * n), tile)
-            res.append(tile)
+    def halo_tiles(k, slot):
+        axis, n = STRIP_PLACE[k]
+        msg = [recv[slot, axis, tile(j, 32 * n)] for j in range(4)]
+        tail = recv[slot, axis, pl.ds(64, 8)]
+        corner = crecv[slot, k // 2]
+        inner = rows_by(corner, 2 * lax.rem(sub, 4) + 1)
+        if k in PRIMARY:
+            tail = jnp.where(halo_lane, lanes_by(inner, primary_back), tail)
+            msg = [jnp.where(lane_s >= 6, pltpu.roll(corner, (6 - 2 * j) % SIZE, 1), msg[j]) for j in range(4)]
+        else:
+            tail = jnp.where(lane_s >= 6, lanes_by(inner, twin_back), tail)
+        res = [roll_rows(msg[i // 4], 6 - 2 * (i % 4)) for i in range(TILES)]
+        for i in range(12, TILES):
+            res[i] = jnp.where(sub == 5, roll_rows(tail, 17 - i - 4 * n), res[i])
         return res
-
-    def own_rows(i):
-        return sub < (6 if i < 12 else 5)
 
     def wait_all(out, slot):
         for axis in (0, 1):
@@ -286,32 +299,31 @@
             corner_copy(k, out, slot).wait()
         strip_copy(2, out, slot).wait()
 
-    def halos_of(slot):
-        halos = {}
-        for k in (1, 3, 5, 0, 2, 4):
-            halos[k] = halo_tiles(k, *STRIP_PLACE[k], slot, k in PRIMARY)
-        return halos
+    inner_edge = halo_lane & (lane_s == 5)
 
     def merge(arrs, k, rows, lanes):
         side = tiles_of(lanes)
         for i in range(TILES):
-            new = arrs[k, 8 * i:8 * i + 8]
+            own_rows = sub < (6 if i < 12 else 5)
             if k in PRIMARY:
-                new = jnp.where(own_rows(i), jnp.where(halo_lane, side[i], new), rows[i])
+                sideways = (halo_lane & own_rows) | (inner_edge & (sub >= 6))
             else:
-                new = jnp.where(halo_lane, side[i], jnp.where(own_rows(i), new, rows[i]))
-            arrs[k, 8 * i:8 * i + 8] = new
+                sideways = halo_lane if i < 12 else halo_lane & ((sub != 5) | inner_edge)
+            arrs[k, tile(i)] = jnp.where(sideways, side[i], jnp.where(own_rows, arrs[k, tile(i)], rows[i]))
+
+    def ghosts_from(dst, src):
+        for k in range(6):
+            near = src[ACROSS[k]]
+            dst[k, row(0)] = near[24:25]
+            dst[k, row(1)] = near[16:17]
 
     def finish(slot):
         wait_all(0, slot)
-        halos = halos_of(slot)
+        halos = {k: halo_tiles(k, slot) for k in (1, 3, 5, 0, 2, 4)}
         lanes = {TWIN[k]: turn(join(halos[k])) for k in (1, 3, 5, 0, 2, 4)}
         for k in (0, 2, 4, 1, 3, 5):
             merge(qa, k, halos[k], lanes[k])
-        for k in range(6):
-            near = ACROSS[k]
-            qa[k, 0:1] = qa[near, 24:25]
-            qa[k, 8:9] = qa[near, 16:17]
+        ghosts_from(qa, [qa[k, pl.ds(0, 32)] for k in range(6)])
 
     def scale_faces(first_step):
         def one(step, carry):
@@ -360,27 +372,24 @@
 
     wait_all(1, 2)
     wait_all(2, 3)
-    wind_halos, side_halos = halos_of(2), halos_of(3)
     for k in range(6):
-        merge(qb, k, wind_halos[k], turn(join(side_halos[TWIN[k]])))
+        merge(qb, k, halo_tiles(k, 2), turn(join(halo_tiles(TWIN[k], 3))))
     for k in range(6):
-        qb[k, 8:9] = -qb[ACROSS[k], 16:17]
+        qb[k, row(1)] = -qb[ACROSS[k], row(2)]
     for k in range(6):
         here = qb[k]
-        after = jnp.concatenate([here[8:], roll_rows(here[:8], -1)], axis=0)
+        after = join([here[8:], roll_rows(here[:8], -1)])
         wf[k] = (0.5 / (6.0 * C_SPEED)) * (here + after)
     scale_faces(0)
 
     def x_part(a_ref, k, faces):
         a = a_ref[k]
-        before = jnp.concatenate([a_ref[k, 119:127], a[:120]], axis=0)
-        after = jnp.concatenate([a[8:], a_ref[k, 1:9]], axis=0)
+        before = join([a_ref[k, tile(15, -1)], a[:-8]])
+        after = join([a[8:], a_ref[k, tile(0, 1)]])
         m = before + after
         v = 8.0 * a - m
-        v_after = jnp.concatenate([v[8:], roll_rows(v[:8], -1)], axis=0)
-        flux = faces * (v + v_after)
-        flux_before = jnp.concatenate([roll_rows(flux[120:], 1), flux[:120]], axis=0)
-        return (m - flux) + flux_before
+        flux = faces * (v + join([v[8:], roll_rows(v[:8], -1)]))
+        return (m - flux) + join([roll_rows(flux[-8:], 1), flux[:-8]])
 
     def parts_of(src, dst, second, step, group):
         part = {}
@@ -408,10 +417,7 @@
             if before_end is not None and pair == (0, 1, 2, 3):
                 before_end()
         if before_end is None:
-            for k in range(6):
-                near = new[ACROSS[k]]
-                dst[k, 0:1] = near[24:25]
-                dst[k, 8:9] = near[16:17]
+            ghosts_from(dst, new)
 
     def run_block(count, slot, before_end):
         finish(slot)

time: 184 us -> 183 us (level)
  no operation moved by 1% of the time
where the time goes in v5:
time: 183 us
  Pallas kernels  181 us (99%)
    pallas_call x1, Pallas kernels, local_run(): pl.pallas_call(functools.partial(kernel, own, steps, axis_names), out_sha...  181 us

profile of v5, /device:TPU:0, one launch (start us, length us, event | category | flops | bytes accessed | tf_op | source)
XLA Modules:
  0.0 182.7 jit_solution(3451294633319830300)
XLA Ops:
  0.0 181.1 %advect.1 = f32[3,90,90]{2,1,0:T(8,128)} custom-call(f32[256]{0:T(256)} %ws_in.1, f32[3,90,90]{2,1,0:T(8,128)} %q_in.1, f32[3,90,90]{2,1,0:T(8,128)} %wa_in.1, f32[3,90,90]{2,1,0:T(8,128)} %wb_in.1, f32[128,128]{1,0:T(8,128)} %constant.2.clone.gain_in), custom_call_target="tpu_custom_call" | custom-call | tf_op jit(solution)/shard_map/advect/pallas_call | solution.py:83
  181.1 1.6 copy.7

commit v6 on v5

--- a/solution.py
+++ b/solution.py
@@ -14,19 +14,17 @@
 MESH = pl.DeviceIdType.MESH
 HIGHEST = lax.Precision.HIGHEST
 
-TWIN = (1, 0, 3, 2, 5, 4)
+TWIN = tuple(k ^ 1 for k in range(6))
 ACROSS = (2, 4, 0, 5, 1, 3)
 PRIMARY = (0, 2, 4)
 STRIPS = ((2, 4), (0, 5), (1, 3))
-STRIP_PLACE = {k: (axis, n) for axis in range(3) for n, k in enumerate(STRIPS[axis])}
+STRIP_PLACE = {k: (axis, n) for axis, pair in enumerate(STRIPS) for n, k in enumerate(pair)}
 CORNERS = {0: (0, 1, 1), 2: (1, 0, 1), 4: (1, 1, 0)}
 
 SIZE = 128
 TILES = 16
-LOW = 2
-OWN = 90
-BLOCK_STEPS = 9
-LANE_ORDER = (8, 7, 9, 6, 10, 5, 11, 4, 12, 3, 13, 2, 14, 1, 15, 0)
+EDGE = 10
+BLOCK_STEPS = 10
 GROUPS = ((0, 2), (1, 3), (4, 5))
 
 
@@ -39,12 +37,15 @@
     return 8 - half + 2 * half * (1 - b % 2)
 
 
-def tile(i, offset=0):
-    return pl.ds(8 * i + offset, 8)
-
-
-def row(i, offset=0):
-    return pl.ds(8 * i + offset, 1)
+LANE_ORDER = tuple(lane_group(b) for b in range(TILES))
+
+
+def tile(i):
+    return pl.ds(8 * i, 8)
+
+
+def row(i, sublane=0):
+    return pl.ds(8 * i + sublane, 1)
 
 
 def tiles_of(arr):
@@ -75,8 +76,8 @@
         dalpha = 0.5 * math.pi / cells
         place = np.arange(SIZE)
         lane_idx = TILES * (place % 8) + lane_group(place // 8)
-        tan_a = np.tan((row_idx(place) - LOW + 0.5) * dalpha - 0.25 * math.pi)[:, None]
-        tan_b = np.tan((lane_idx - LOW + 0.5) * dalpha - 0.25 * math.pi)[None, :]
+        tan_a = np.tan((row_idx(place) + 0.5) * dalpha - 0.25 * math.pi)[:, None]
+        tan_b = np.tan((lane_idx + 0.5) * dalpha - 0.25 * math.pi)[None, :]
         r_sq = 1.0 + tan_a * tan_a + tan_b * tan_b
         inv_sqrt_g = r_sq * np.sqrt(r_sq) / ((1.0 + tan_a * tan_a) * (1.0 + tan_b * tan_b))
         gain = (0.5 * C_SPEED * CFL_STEP * inv_sqrt_g).astype(np.float32)
@@ -92,19 +93,15 @@
                 pltpu.VMEM((6, SIZE, SIZE), jnp.float32),
                 pltpu.VMEM((BLOCK_STEPS, 6, SIZE, SIZE), jnp.float32),
                 pltpu.VMEM((6, SIZE, SIZE), jnp.float32),
+                pltpu.VMEM((6, 8, SIZE), jnp.float32),
                 pltpu.VMEM((4, SIZE, SIZE), jnp.float32),
                 pltpu.VMEM((3, 3, own, own), jnp.float32),
                 pltpu.VMEM((3, own, own), jnp.float32),
-                pltpu.VMEM((3, 3, 72, SIZE), jnp.float32),
-                pltpu.VMEM((4, 3, 72, SIZE), jnp.float32),
-                pltpu.VMEM((3, 3, 8, SIZE), jnp.float32),
-                pltpu.VMEM((4, 3, 8, SIZE), jnp.float32),
-                pltpu.SemaphoreType.DMA((4, 6)),
-                pltpu.SemaphoreType.DMA((4, 6)),
-                pltpu.SemaphoreType.DMA((3, 3)),
-                pltpu.SemaphoreType.DMA((3, 3)),
-                pltpu.SemaphoreType.DMA((3,)),
-                pltpu.SemaphoreType.DMA((3,)),
+                pltpu.VMEM((3, 6, 40, SIZE), jnp.float32),
+                pltpu.VMEM((4, 6, 40, SIZE), jnp.float32),
+                pltpu.VMEM((3, 3, 16, SIZE), jnp.float32),
+                pltpu.VMEM((4, 3, 16, SIZE), jnp.float32),
+            ] + [pltpu.SemaphoreType.DMA(shape) for shape in ((4, 6), (3, 3), (3,)) for _ in range(2)] + [
                 pltpu.SemaphoreType.DMA((5,)),
             ],
             compiler_params=pltpu.CompilerParams(collective_id=0, has_side_effects=True),
@@ -119,7 +116,7 @@
 
 
 def kernel(own, steps, axis_names, ws_in, q_in, wa_in, wb_in, gain_in, out_ref,
-           ws_ref, fields, qa, qb, sw, wf, coef, tiles, result, send, recv, csend, crecv,
+           ws_ref, fields, qa, qb, sw, wf, wlast, coef, tiles, result, send, recv, csend, crecv,
            ssem, rsem, tsend, trecv, osend, orecv, isem):
     tx, ty, core = lax.axis_index('tx'), lax.axis_index('ty'), lax.axis_index('panel')
     by, bz, bx = tx, ty, lax.rem(core + tx + 1, 2)
@@ -176,10 +173,9 @@
                 tiles[f, quad] = fields[f, slot]
 
     def placing(shape, spot_axis, to_idx, flip):
-        dist = to_idx(lax.broadcasted_iota(jnp.int32, shape, spot_axis)) - LOW
+        dist = to_idx(lax.broadcasted_iota(jnp.int32, shape, spot_axis))
         cell = lax.broadcasted_iota(jnp.int32, shape, 1 - spot_axis)
-        inside = (dist >= 0) & (dist < own)
-        source = jnp.where(inside, jnp.where(flip == 1, own - 1 - dist, dist), -1)
+        source = jnp.where(dist < own, jnp.where(flip == 1, own - 1 - dist, dist), -1)
         return jnp.where(source == cell, 1.0, 0.0)
 
     def row_to_idx(row):
@@ -198,22 +194,19 @@
     sub = lax.broadcasted_iota(jnp.int32, (8, SIZE), 0)
     lane = lax.broadcasted_iota(jnp.int32, (8, SIZE), 1)
     lane_s, lane_i = lax.rem(lane, 8), lax.rem(lane_to_idx(lane), TILES)
-    halo_lane = (lane_s >= 6) | ((lane_s == 5) & (lane_i >= 12))
+    edge_lane = (lane_s == 5) & (lane_i >= EDGE)
+    halo_lane = (lane_s >= 6) | edge_lane
 
     def mirror_lane(number):
-        return jnp.where(lane_i < 8, 8 * (1 + 2 * lane_i) + 11 - number, 8 * (30 - 2 * lane_i) + 10 - number)
-
-    odd_row, odd_lane = lax.rem(sub, 2), lax.rem(lane, 2)
-    pair_src = mirror_lane(6 + odd_lane)
+        there = lax.rem(19 - lane_i, TILES)
+        group = jnp.where(there < 8, 15 - 2 * there, 2 * there - TILES)
+        return 8 * group + jnp.where(lane_i < 4, 11, EDGE) - number
+
+    odd_row = lax.rem(sub, 2)
+    pair_src = mirror_lane(6 + lax.rem(lane, 2))
+    twin_src = jnp.where(lane_s < 2, mirror_lane(6 + lane_s), 0)
+    tail_src = jnp.where(halo_lane, mirror_lane(lane_s), 0)
     row_pair, lane_pair = sub // 2, lane_s // 2
-    late_group = lane_i >= 14
-    from_twin = (lane_pair == 2) | ((lane_pair == 3) & jnp.logical_not(late_group))
-    twin_src = jnp.where(from_twin, mirror_lane(4 + lane_pair), 0)
-    inner_src = jnp.where(lane_pair == 3, mirror_lane(5), 8 * (34 - 2 * lane_i) + 5)
-    primary_src = jnp.where(from_twin, 0, jnp.where((lane_pair > 0) & late_group, inner_src, mirror_lane(6 + lane_pair)))
-    inner_lane = jnp.where(late_group, 16 * lane_i - 121, 16 * lane_i - 93)
-    primary_back = jnp.where(lane_s == 6, lane - 5, jnp.where(lane_s == 7, lane - 4, jnp.where(halo_lane, inner_lane, 0)))
-    twin_back = jnp.where(lane_s == 6, lane - 1, lane)
 
     def rows_by(arr, idx):
         return jnp.take_along_axis(arr, idx, axis=0, mode="promise_in_bounds")
@@ -222,9 +215,9 @@
         return jnp.take_along_axis(arr, idx, axis=1, mode="promise_in_bounds")
 
     def by_number(number, parts):
-        res = parts[3]
-        for m in (2, 1, 0):
-            res = jnp.where(number == m, parts[m], res)
+        res = parts[0]
+        for m, part in enumerate(parts):
+            res = jnp.where(number == m, part, res) if m else res
         return res
 
     def peer(mirrored):
@@ -232,7 +225,7 @@
 
     def strip_copy(axis, out, slot):
         return pltpu.make_async_remote_copy(
-            send.at[out, axis], recv.at[slot, axis], ssem.at[slot, axis], rsem.at[slot, axis],
+            send.at[out, pl.ds(2 * axis, 2)], recv.at[slot, pl.ds(2 * axis, 2)], ssem.at[slot, axis], rsem.at[slot, axis],
             device_id=peer(tuple(int(n == axis) for n in range(3))), device_id_type=MESH)
 
     def corner_copy(k, out, slot):
@@ -247,23 +240,25 @@
     def pack(arrs, k, out, sign):
         axis, n = STRIP_PLACE[k]
         a = tiles_of(arrs[k])
-        msg = []
-        for j in range(4):
-            first, sublane = (7, 5 - odd_row) if j < 2 else (23, 4 - odd_row)
-            msg.append(signed(sign, by_number(row_pair, [rows_by(a[first - 4 * j - m], sublane) for m in range(4)])))
-        tail = signed(sign, by_number(lax.rem(sub, 4), [rows_by(a[11 - m], 5 + 0 * sub) for m in range(4)]))
-        send[out, axis, pl.ds(32 * n, 32)] = join(msg)
-        send[out, axis, pl.ds(64 + 4 * n, 4)] = tail[4 * n:4 * n + 4]
-        return msg, tail
+
+        def mirrored(i, sublane):
+            return rows_by(a[(19 - i) % TILES], sublane)
+
+        msg = [by_number(row_pair, [mirrored(i, (5 if i < 4 else 4) - odd_row) for i in range(4 * j, 4 * j + 4)])
+               for j in range(4)]
+        tail = [mirrored(i, 5 + 0 * sub) for i in range(EDGE, TILES)] + [mirrored(i, 3 + 0 * sub) for i in range(2)]
+        msg = [signed(sign, part) for part in msg + [by_number(sub, tail)]]
+        send[out, 2 * axis + n] = join(msg)
+        return msg
 
     def pack_pair(arrs, k, out, sign, corner_sign, twin_tail):
-        msg, tail = pack(arrs, k, out, sign)
+        *msg, tail = pack(arrs, k, out, sign)
         pairs = by_number(lane_pair, [lanes_by(m, pair_src) for m in msg])
-        inner = jnp.where(from_twin, lanes_by(rows_by(twin_tail, row_pair), twin_src), lanes_by(rows_by(tail, row_pair), primary_src))
-        csend[out, PRIMARY.index(k)] = signed(corner_sign, jnp.where(odd_row * odd_lane == 1, inner, pairs))
+        near = jnp.where(lane_s < 2, lanes_by(twin_tail, twin_src), lanes_by(tail, tail_src))
+        csend[out, k // 2] = signed(corner_sign, join([pairs, near]))
 
     def start_first(arrs, out, slot, sign, corner_sign):
-        tails = [pack(arrs, k, out, sign)[1] for k in (1, 3)]
+        tails = [pack(arrs, k, out, sign)[-1] for k in (1, 3)]
         strip_copy(2, out, slot).start()
         for k, tail in zip((0, 2), tails):
             pack_pair(arrs, k, out, sign, corner_sign, tail)
@@ -271,25 +266,26 @@
             corner_copy(k, out, slot).start()
 
     def start_rest(arrs, out, slot, sign, corner_sign):
-        pack_pair(arrs, 4, out, sign, corner_sign, pack(arrs, 5, out, sign)[1])
+        pack_pair(arrs, 4, out, sign, corner_sign, pack(arrs, 5, out, sign)[-1])
         corner_copy(4, out, slot).start()
         strip_copy(1, out, slot).start()
         strip_copy(0, out, slot).start()
 
+    def strip(k, slot):
+        axis, n = STRIP_PLACE[k]
+        return tiles_of(recv[slot, 2 * axis + n])
+
     def halo_tiles(k, slot):
-        axis, n = STRIP_PLACE[k]
-        msg = [recv[slot, axis, tile(j, 32 * n)] for j in range(4)]
-        tail = recv[slot, axis, pl.ds(64, 8)]
-        corner = crecv[slot, k // 2]
-        inner = rows_by(corner, 2 * lax.rem(sub, 4) + 1)
+        *msg, tail = strip(k, slot)
+        pairs, near = tiles_of(crecv[slot, k // 2])
         if k in PRIMARY:
-            tail = jnp.where(halo_lane, lanes_by(inner, primary_back), tail)
-            msg = [jnp.where(lane_s >= 6, pltpu.roll(corner, (6 - 2 * j) % SIZE, 1), msg[j]) for j in range(4)]
+            tail = jnp.where(halo_lane, near, tail)
+            msg = [jnp.where(lane_s >= 6, pltpu.roll(pairs, (6 - 2 * j) % SIZE, 1), msg[j]) for j in range(4)]
         else:
-            tail = jnp.where(lane_s >= 6, lanes_by(inner, twin_back), tail)
+            tail = jnp.where(lane_s >= 6, pltpu.roll(near, 6, 1), tail)
         res = [roll_rows(msg[i // 4], 6 - 2 * (i % 4)) for i in range(TILES)]
-        for i in range(12, TILES):
-            res[i] = jnp.where(sub == 5, roll_rows(tail, 17 - i - 4 * n), res[i])
+        for i in range(EDGE, TILES):
+            res[i] = jnp.where(sub == 5, roll_rows(tail, 15 - i), res[i])
         return res
 
     def wait_all(out, slot):
@@ -299,23 +295,15 @@
             corner_copy(k, out, slot).wait()
         strip_copy(2, out, slot).wait()
 
-    inner_edge = halo_lane & (lane_s == 5)
-
     def merge(arrs, k, rows, lanes):
         side = tiles_of(lanes)
         for i in range(TILES):
-            own_rows = sub < (6 if i < 12 else 5)
+            own_rows = sub < (6 if i < EDGE else 5)
             if k in PRIMARY:
-                sideways = (halo_lane & own_rows) | (inner_edge & (sub >= 6))
+                sideways = (halo_lane & own_rows) | (edge_lane & (sub >= 6))
             else:
-                sideways = halo_lane if i < 12 else halo_lane & ((sub != 5) | inner_edge)
+                sideways = halo_lane if i < EDGE else halo_lane & ((sub != 5) | edge_lane)
             arrs[k, tile(i)] = jnp.where(sideways, side[i], jnp.where(own_rows, arrs[k, tile(i)], rows[i]))
-
-    def ghosts_from(dst, src):
-        for k in range(6):
-            near = src[ACROSS[k]]
-            dst[k, row(0)] = near[24:25]
-            dst[k, row(1)] = near[16:17]
 
     def finish(slot):
         wait_all(0, slot)
@@ -323,7 +311,6 @@
         lanes = {TWIN[k]: turn(join(halos[k])) for k in (1, 3, 5, 0, 2, 4)}
         for k in (0, 2, 4, 1, 3, 5):
             merge(qa, k, halos[k], lanes[k])
-        ghosts_from(qa, [qa[k, pl.ds(0, 32)] for k in range(6)])
 
     def scale_faces(first_step):
         def one(step, carry):
@@ -375,26 +362,41 @@
     for k in range(6):
         merge(qb, k, halo_tiles(k, 2), turn(join(halo_tiles(TWIN[k], 3))))
     for k in range(6):
-        qb[k, row(1)] = -qb[ACROSS[k], row(2)]
-    for k in range(6):
         here = qb[k]
+        scaled = 0.5 / (6.0 * C_SPEED)
         after = join([here[8:], roll_rows(here[:8], -1)])
-        wf[k] = (0.5 / (6.0 * C_SPEED)) * (here + after)
+        beyond = jnp.where(sub == 7, roll_rows(strip(k, 2)[-1], 1), after[-8:])
+        wf[k] = scaled * (here + after)
+        wf[k, row(15, 7)] = scaled * (here[:1] - qb[ACROSS[k], row(0)])
+        wlast[k] = scaled * (here[-8:] + beyond)
     scale_faces(0)
 
-    def x_part(a_ref, k, faces):
+    def x_part(a_ref, k, faces, ghosts=False, beyond=None):
         a = a_ref[k]
-        before = join([a_ref[k, tile(15, -1)], a[:-8]])
-        after = join([a[8:], a_ref[k, tile(0, 1)]])
-        m = before + after
+        first, last = a[:8], a[-8:]
+        below, above = roll_rows(last, 1), roll_rows(first, -1)
+        if ghosts:
+            below = jnp.where(sub == 0, a_ref[ACROSS[k], tile(0)], below)
+        if beyond is not None:
+            above = jnp.where(sub == 7, roll_rows(beyond[0], 1), above)
+        m = join([below, a[:-8]]) + join([a[8:], above])
         v = 8.0 * a - m
-        flux = faces * (v + join([v[8:], roll_rows(v[:8], -1)]))
-        return (m - flux) + join([roll_rows(flux[-8:], 1), flux[:-8]])
-
-    def parts_of(src, dst, second, step, group):
+        v_above, here = roll_rows(v[:8], -1), faces
+        if beyond is not None:
+            v_above = 8.0 * above - (last + jnp.where(sub == 7, beyond[0], roll_rows(a[8:16], -1)))
+            here = join([faces[:-8], beyond[1]])
+        flux = here * (v + join([v[8:], v_above]))
+        flux_below = roll_rows(flux[-8:], 1)
+        if ghosts:
+            v_below = 8.0 * below - (jnp.where(sub == 0, a_ref[ACROSS[k], tile(1)], roll_rows(a[-16:-8], 1)) + first)
+            flux_below = roll_rows(faces[-8:], 1) * (v_below + v[:8])
+        return (m - flux) + join([flux_below, flux[:-8]])
+
+    def parts_of(src, dst, second, step, group, ghosts, scale, slot):
         part = {}
         for k in group:
-            part[k] = coef[2 if second else 0] * x_part(src, k, sw[step, k])
+            beyond = None if scale is None else (strip(k, slot)[-1], scale * wlast[k])
+            part[k] = coef[2 if second else 0] * x_part(src, k, sw[step, k], ghosts, beyond)
             if k in PRIMARY:
                 own_part = coef[3 if second else 1] * src[k]
                 if second:
@@ -402,10 +404,10 @@
                 part[k] = own_part + part[k]
         return part, {k: turn(part[k]) for k in group}
 
-    def stage(src, dst, second, step, before_end=None):
+    def stage(src, dst, second, step, ghosts=False, scale=None, slot=None, before_end=None):
         part, turned = {}, {}
         for group in GROUPS:
-            more = parts_of(src, dst, second, step, group)
+            more = parts_of(src, dst, second, step, group, ghosts, scale, slot)
             part.update(more[0])
             turned.update(more[1])
         new = {}
@@ -416,18 +418,23 @@
                 dst[k] = new[k]
             if before_end is not None and pair == (0, 1, 2, 3):
                 before_end()
-        if before_end is None:
-            ghosts_from(dst, new)
-
-    def run_block(count, slot, before_end):
+        if before_end is None and scale is None:
+            for k in range(6):
+                near = new[ACROSS[k]]
+                dst[k, row(14, 7)] = near[8:9]
+                dst[k, row(15, 7)] = near[:1]
+
+    def run_block(first_step, count, slot, before_end):
         finish(slot)
+        stage(qa, qb, False, 0, ghosts=True, scale=ws_ref[first_step], slot=slot)
+        stage(qb, qa, True, 0, ghosts=True)
 
         def one_step(step, carry):
             stage(qa, qb, False, step)
             stage(qb, qa, True, step)
             return carry
 
-        lax.fori_loop(0, count - 1, one_step, 0, unroll=True)
+        lax.fori_loop(1, count - 1, one_step, 0, unroll=True)
         stage(qa, qb, False, count - 1)
         stage(qb, qa, True, count - 1, before_end=before_end)
 
@@ -435,13 +442,13 @@
 
     def block(blk, carry):
         out_slot = lax.rem(blk + 1, 2)
-        run_block(BLOCK_STEPS, lax.rem(blk, 2), functools.partial(start_first, qa, 0, out_slot, 1.0, 1.0))
+        run_block(blk * BLOCK_STEPS, BLOCK_STEPS, lax.rem(blk, 2), functools.partial(start_first, qa, 0, out_slot, 1.0, 1.0))
         start_rest(qa, 0, out_slot, 1.0, 1.0)
         scale_faces((blk + 1) * BLOCK_STEPS)
         return carry
 
     lax.fori_loop(0, full_blocks, block, 0)
-    run_block(steps - full_blocks * BLOCK_STEPS, full_blocks % 2, lambda: None)
+    run_block(full_blocks * BLOCK_STEPS, steps - full_blocks * BLOCK_STEPS, full_blocks % 2, lambda: None)
 
     def result_copy(quad, slot, device, number):
         return pltpu.make_async_remote_copy(

time: 183 us -> 179 us (0.978)
  Pallas kernels: 181 us -> 178 us
    pallas_call x1, Pallas kernels: 181 us -> 178 us  [local_run(): pl.pallas_call(functools.partial(kernel, own, steps, axis_names), out_sha...]
where the time goes in v6:
time: 179 us
  Pallas kernels  178 us (99%)
    pallas_call x1, Pallas kernels, local_run(): pl.pallas_call(functools.partial(kernel, own, steps, axis_names), out_sha...  178 us

profile of v6, /device:TPU:0, one launch (start us, length us, event | category | flops | bytes accessed | tf_op | source)
XLA Modules:
  0.0 179.2 jit_solution(13215369802418936339)
XLA Ops:
  0.0 177.6 %advect.1 = f32[3,90,90]{2,1,0:T(8,128)} custom-call(f32[256]{0:T(256)} %ws_in.1, f32[3,90,90]{2,1,0:T(8,128)} %q_in.1, f32[3,90,90]{2,1,0:T(8,128)} %wa_in.1, f32[3,90,90]{2,1,0:T(8,128)} %wb_in.1, f32[128,128]{1,0:T(8,128)} %constant.2.clone.gain_in), custom_call_target="tpu_custom_call" | custom-call | tf_op jit(solution)/shard_map/advect/pallas_call | solution.py:84
  177.6 1.6 copy.7

commit v7 on v6

--- a/solution.py
+++ b/solution.py
@@ -19,7 +19,7 @@
 PRIMARY = (0, 2, 4)
 STRIPS = ((2, 4), (0, 5), (1, 3))
 STRIP_PLACE = {k: (axis, n) for axis, pair in enumerate(STRIPS) for n, k in enumerate(pair)}
-CORNERS = {0: (0, 1, 1), 2: (1, 0, 1), 4: (1, 1, 0)}
+CORNERS = {1: (0, 1, 1), 3: (1, 0, 1), 4: (1, 1, 0)}
 
 SIZE = 128
 TILES = 16
@@ -99,8 +99,8 @@
                 pltpu.VMEM((3, own, own), jnp.float32),
                 pltpu.VMEM((3, 6, 40, SIZE), jnp.float32),
                 pltpu.VMEM((4, 6, 40, SIZE), jnp.float32),
-                pltpu.VMEM((3, 3, 16, SIZE), jnp.float32),
-                pltpu.VMEM((4, 3, 16, SIZE), jnp.float32),
+                pltpu.VMEM((3, 3, 8, SIZE), jnp.float32),
+                pltpu.VMEM((4, 3, 8, SIZE), jnp.float32),
             ] + [pltpu.SemaphoreType.DMA(shape) for shape in ((4, 6), (3, 3), (3,)) for _ in range(2)] + [
                 pltpu.SemaphoreType.DMA((5,)),
             ],
@@ -197,16 +197,30 @@
     edge_lane = (lane_s == 5) & (lane_i >= EDGE)
     halo_lane = (lane_s >= 6) | edge_lane
 
-    def mirror_lane(number):
-        there = lax.rem(19 - lane_i, TILES)
-        group = jnp.where(there < 8, 15 - 2 * there, 2 * there - TILES)
-        return 8 * group + jnp.where(lane_i < 4, 11, EDGE) - number
+    def group_lane(group, number):
+        return 8 * jnp.where(group < 8, 15 - 2 * group, 2 * group - TILES) + number
+
+    def mirror_lane(group, number):
+        return group_lane(lax.rem(19 - group, TILES), jnp.where(group < 4, 11, EDGE) - number)
 
     odd_row = lax.rem(sub, 2)
-    pair_src = mirror_lane(6 + lax.rem(lane, 2))
-    twin_src = jnp.where(lane_s < 2, mirror_lane(6 + lane_s), 0)
-    tail_src = jnp.where(halo_lane, mirror_lane(lane_s), 0)
     row_pair, lane_pair = sub // 2, lane_s // 2
+    high, mid = lane_i >= EDGE, (lane_i >= 4) & (lane_i < EDGE)
+    edge_group = jnp.where(mid, lane_i + 6, lane_i)
+    at_edge = ((lane_s == 5) | (lane_s == 7)) & (high | mid)
+    source_vreg = jnp.where(at_edge, jnp.where(lane_s == 7, 0, 2) + jnp.where(high, 0, 1), lane_pair)
+    source_lane = jnp.where(at_edge, mirror_lane(edge_group, 5), mirror_lane(lane_i, 6 + lax.rem(lane, 2)))
+    at_four = lane_s == 4
+    takes_first = (odd_row == 1) & ((lane_s == 1) | (lane_s == 3) | (at_four & high))
+    takes_last = (odd_row == 1) & ((lane_s == 6) | (at_four & mid))
+    first_src = jnp.where(takes_first, mirror_lane(lane_i, jnp.where(at_four, 5, 6 + lane_s // 2)), 0)
+    last_src = jnp.where(takes_last, mirror_lane(jnp.where(at_four, edge_group, lane_i), jnp.where(at_four, 5, 6 + sub // 4)), 0)
+    low_group = lane_i - 6
+    edge_back = [group_lane(lane_i, 7), group_lane(low_group, 7), group_lane(lane_i, 5), group_lane(low_group, 5)]
+    msg_back = [jnp.where(lane_s >= 6, lane - 6 + 2 * j, jnp.where(edge_lane, edge_back[j], 0)) for j in range(4)]
+    first_back = jnp.where(lane_s >= 6, lane + lane_s - 11, jnp.where(edge_lane, lane - 1, 0))
+    last_back = jnp.where(lane_s >= 6, lane - lane_s + 6, jnp.where(edge_lane, group_lane(low_group, 4), 0))
+    last_row = 1 + 2 * jnp.where((sub >= 4) & (lane_s < 7), odd_row, lax.rem(sub + 2 * (sub // 4), 4))
 
     def rows_by(arr, idx):
         return jnp.take_along_axis(arr, idx, axis=0, mode="promise_in_bounds")
@@ -229,7 +243,7 @@
             device_id=peer(tuple(int(n == axis) for n in range(3))), device_id_type=MESH)
 
     def corner_copy(k, out, slot):
-        n = PRIMARY.index(k)
+        n = k // 2
         return pltpu.make_async_remote_copy(
             csend.at[out, n], crecv.at[slot, n], ssem.at[slot, 3 + n], rsem.at[slot, 3 + n],
             device_id=peer(CORNERS[k]), device_id_type=MESH)
@@ -251,25 +265,31 @@
         send[out, 2 * axis + n] = join(msg)
         return msg
 
-    def pack_pair(arrs, k, out, sign, corner_sign, twin_tail):
-        *msg, tail = pack(arrs, k, out, sign)
-        pairs = by_number(lane_pair, [lanes_by(m, pair_src) for m in msg])
-        near = jnp.where(lane_s < 2, lanes_by(twin_tail, twin_src), lanes_by(tail, tail_src))
-        csend[out, k // 2] = signed(corner_sign, join([pairs, near]))
-
-    def start_first(arrs, out, slot, sign, corner_sign):
-        tails = [pack(arrs, k, out, sign)[-1] for k in (1, 3)]
+    def pack_corner(k, packed, out, corner_sign):
+        *msg, tail = packed
+        block = by_number(source_vreg, [lanes_by(m, source_lane) for m in msg])
+        first = lanes_by(rows_by(tail, row_pair), first_src)
+        last = lanes_by(rows_by(tail, 4 + lax.rem(row_pair, 2)), last_src)
+        block = jnp.where(takes_first, first, jnp.where(takes_last, last, block))
+        csend[out, k // 2] = signed(corner_sign, block)
+
+    def sender(arrs, out, slot, sign=1.0, corner_sign=1.0):
+        packed = [pack(arrs, k, out, sign) for k in (1, 3)]
         strip_copy(2, out, slot).start()
-        for k, tail in zip((0, 2), tails):
-            pack_pair(arrs, k, out, sign, corner_sign, tail)
+        for k, msg in zip((1, 3), packed):
+            pack_corner(k, msg, out, corner_sign)
+        for k in (1, 3):
+            corner_copy(k, out, slot).start()
+        yield
         for k in (0, 2):
-            corner_copy(k, out, slot).start()
-
-    def start_rest(arrs, out, slot, sign, corner_sign):
-        pack_pair(arrs, 4, out, sign, corner_sign, pack(arrs, 5, out, sign)[-1])
+            pack(arrs, k, out, sign)
+        yield
+        pack_corner(4, pack(arrs, 4, out, sign), out, corner_sign)
         corner_copy(4, out, slot).start()
+        pack(arrs, 5, out, sign)
         strip_copy(1, out, slot).start()
         strip_copy(0, out, slot).start()
+        yield
 
     def strip(k, slot):
         axis, n = STRIP_PLACE[k]
@@ -277,12 +297,11 @@
 
     def halo_tiles(k, slot):
         *msg, tail = strip(k, slot)
-        pairs, near = tiles_of(crecv[slot, k // 2])
-        if k in PRIMARY:
-            tail = jnp.where(halo_lane, near, tail)
-            msg = [jnp.where(lane_s >= 6, pltpu.roll(pairs, (6 - 2 * j) % SIZE, 1), msg[j]) for j in range(4)]
-        else:
-            tail = jnp.where(lane_s >= 6, pltpu.roll(near, 6, 1), tail)
+        if k in CORNERS:
+            block = crecv[slot, k // 2]
+            msg = [jnp.where(halo_lane, lanes_by(block, msg_back[j]), msg[j]) for j in range(4)]
+            last = rows_by(lanes_by(block, last_back), last_row)
+            tail = jnp.where(halo_lane, jnp.where(sub < 4, rows_by(lanes_by(block, first_back), last_row), last), tail)
         res = [roll_rows(msg[i // 4], 6 - 2 * (i % 4)) for i in range(TILES)]
         for i in range(EDGE, TILES):
             res[i] = jnp.where(sub == 5, roll_rows(tail, 15 - i), res[i])
@@ -291,7 +310,7 @@
     def wait_all(out, slot):
         for axis in (0, 1):
             strip_copy(axis, out, slot).wait()
-        for k in (2, 4, 0):
+        for k in (3, 4, 1):
             corner_copy(k, out, slot).wait()
         strip_copy(2, out, slot).wait()
 
@@ -299,16 +318,13 @@
         side = tiles_of(lanes)
         for i in range(TILES):
             own_rows = sub < (6 if i < EDGE else 5)
-            if k in PRIMARY:
-                sideways = (halo_lane & own_rows) | (edge_lane & (sub >= 6))
-            else:
-                sideways = halo_lane if i < EDGE else halo_lane & ((sub != 5) | edge_lane)
+            sideways = halo_lane & own_rows if k in CORNERS else halo_lane
             arrs[k, tile(i)] = jnp.where(sideways, side[i], jnp.where(own_rows, arrs[k, tile(i)], rows[i]))
 
     def finish(slot):
         wait_all(0, slot)
-        halos = {k: halo_tiles(k, slot) for k in (1, 3, 5, 0, 2, 4)}
-        lanes = {TWIN[k]: turn(join(halos[k])) for k in (1, 3, 5, 0, 2, 4)}
+        halos = {k: halo_tiles(k, slot) for k in (0, 2, 5, 1, 3, 4)}
+        lanes = {TWIN[k]: turn(join(halos[k])) for k in (0, 2, 5, 1, 3, 4)}
         for k in (0, 2, 4, 1, 3, 5):
             merge(qa, k, halos[k], lanes[k])
 
@@ -346,12 +362,9 @@
                 sw[0, plain] = loc
                 qb[turned] = turn(loc)
         if f == 2:
-            start_first(qb, 1, 2, -1.0, 1.0)
-            start_rest(qb, 1, 2, -1.0, 1.0)
-            start_first(sw.at[0], 2, 3, 1.0, -1.0)
-            start_rest(sw.at[0], 2, 3, 1.0, -1.0)
-    start_first(qa, 0, 0, 1.0, 1.0)
-    start_rest(qa, 0, 0, 1.0, 1.0)
+            list(sender(qb, 1, 2, sign=-1.0))
+            list(sender(sw.at[0], 2, 3, corner_sign=-1.0))
+    list(sender(qa, 0, 0))
 
     coef[1] = 1.0 - 4.0 * coef[0]
     coef[2] = 0.5 * coef[0]
@@ -404,27 +417,27 @@
                 part[k] = own_part + part[k]
         return part, {k: turn(part[k]) for k in group}
 
-    def stage(src, dst, second, step, ghosts=False, scale=None, slot=None, before_end=None):
+    def stage(src, dst, second, step, ghosts=False, scale=None, slot=None, sends=None):
         part, turned = {}, {}
         for group in GROUPS:
             more = parts_of(src, dst, second, step, group, ghosts, scale, slot)
             part.update(more[0])
             turned.update(more[1])
         new = {}
-        for pair in ((0, 1, 2, 3), (4, 5)):
-            for k in pair:
+        for group in ((1, 3), (0, 2), (4, 5)):
+            for k in group:
                 new[k] = part[k] + turned[TWIN[k]]
-            for k in pair:
+            for k in group:
                 dst[k] = new[k]
-            if before_end is not None and pair == (0, 1, 2, 3):
-                before_end()
-        if before_end is None and scale is None:
+            if sends is not None:
+                next(sends)
+        if sends is None and scale is None:
             for k in range(6):
                 near = new[ACROSS[k]]
                 dst[k, row(14, 7)] = near[8:9]
                 dst[k, row(15, 7)] = near[:1]
 
-    def run_block(first_step, count, slot, before_end):
+    def run_block(first_step, count, slot, sends):
         finish(slot)
         stage(qa, qb, False, 0, ghosts=True, scale=ws_ref[first_step], slot=slot)
         stage(qb, qa, True, 0, ghosts=True)
@@ -436,19 +449,18 @@
 
         lax.fori_loop(1, count - 1, one_step, 0, unroll=True)
         stage(qa, qb, False, count - 1)
-        stage(qb, qa, True, count - 1, before_end=before_end)
+        stage(qb, qa, True, count - 1, sends=sends)
 
     full_blocks = (steps - 1) // BLOCK_STEPS
 
     def block(blk, carry):
         out_slot = lax.rem(blk + 1, 2)
-        run_block(blk * BLOCK_STEPS, BLOCK_STEPS, lax.rem(blk, 2), functools.partial(start_first, qa, 0, out_slot, 1.0, 1.0))
-        start_rest(qa, 0, out_slot, 1.0, 1.0)
+        run_block(blk * BLOCK_STEPS, BLOCK_STEPS, lax.rem(blk, 2), sender(qa, 0, out_slot))
         scale_faces((blk + 1) * BLOCK_STEPS)
         return carry
 
     lax.fori_loop(0, full_blocks, block, 0)
-    run_block(full_blocks * BLOCK_STEPS, steps - full_blocks * BLOCK_STEPS, full_blocks % 2, lambda: None)
+    run_block(full_blocks * BLOCK_STEPS, steps - full_blocks * BLOCK_STEPS, full_blocks % 2, iter(range(3)))
 
     def result_copy(quad, slot, device, number):
         return pltpu.make_async_remote_copy(

time: 179 us -> 176 us (0.983)
  Pallas kernels: 178 us -> 175 us
    pallas_call x1, Pallas kernels: 178 us -> 175 us  [local_run(): pl.pallas_call(functools.partial(kernel, own, steps, axis_names), out_sha...]
where the time goes in v7:
time: 176 us
  Pallas kernels  175 us (99%)
    pallas_call x1, Pallas kernels, local_run(): pl.pallas_call(functools.partial(kernel, own, steps, axis_names), out_sha...  175 us

profile of v7, /device:TPU:0, one launch (start us, length us, event | category | flops | bytes accessed | tf_op | source)
XLA Modules:
  0.0 176.3 jit_solution(17341202398614657264)
XLA Ops:
  0.0 174.7 %advect.1 = f32[3,90,90]{2,1,0:T(8,128)} custom-call(f32[256]{0:T(256)} %ws_in.1, f32[3,90,90]{2,1,0:T(8,128)} %q_in.1, f32[3,90,90]{2,1,0:T(8,128)} %wa_in.1, f32[3,90,90]{2,1,0:T(8,128)} %wb_in.1, f32[128,128]{1,0:T(8,128)} %constant.2.clone.gain_in), custom_call_target="tpu_custom_call" | custom-call | tf_op jit(solution)/shard_map/advect/pallas_call | solution.py:84
  174.7 1.6 copy.7

commit v8 on v7

--- a/solution.py
+++ b/solution.py
@@ -23,6 +23,8 @@
 
 SIZE = 128
 TILES = 16
+PITCH = SIZE + 16
+CENTRE = 5
 EDGE = 10
 BLOCK_STEPS = 10
 GROUPS = ((0, 2), (1, 3), (4, 5))
@@ -34,10 +36,10 @@
 
 def lane_group(b):
     half = (b + 1) // 2
-    return 8 - half + 2 * half * (1 - b % 2)
-
-
-LANE_ORDER = tuple(lane_group(b) for b in range(TILES))
+    return np.where(b > 2 * CENTRE, b, CENTRE - half + 2 * half * (1 - b % 2))
+
+
+LANE_ORDER = tuple(int(lane_group(b)) for b in range(TILES))
 
 
 def tile(i):
@@ -89,8 +91,8 @@
             scratch_shapes=[
                 pltpu.SMEM((steps,), jnp.float32),
                 pltpu.VMEM((3, 3, own, own), jnp.float32),
-                pltpu.VMEM((6, SIZE, SIZE), jnp.float32),
-                pltpu.VMEM((6, SIZE, SIZE), jnp.float32),
+                pltpu.VMEM((6, PITCH, SIZE), jnp.float32),
+                pltpu.VMEM((6, PITCH, SIZE), jnp.float32),
                 pltpu.VMEM((BLOCK_STEPS, 6, SIZE, SIZE), jnp.float32),
                 pltpu.VMEM((6, SIZE, SIZE), jnp.float32),
                 pltpu.VMEM((6, 8, SIZE), jnp.float32),
@@ -116,10 +118,11 @@
 
 
 def kernel(own, steps, axis_names, ws_in, q_in, wa_in, wb_in, gain_in, out_ref,
-           ws_ref, fields, qa, qb, sw, wf, wlast, coef, tiles, result, send, recv, csend, crecv,
+           ws_ref, fields, qa_rows, qb_rows, sw, wf, wlast, coef, tiles, result, send, recv, csend, crecv,
            ssem, rsem, tsend, trecv, osend, orecv, isem):
     tx, ty, core = lax.axis_index('tx'), lax.axis_index('ty'), lax.axis_index('panel')
     by, bz, bx = tx, ty, lax.rem(core + tx + 1, 2)
+    qa, qb = (rows.at[:, pl.ds(0, SIZE)] for rows in (qa_rows, qb_rows))
 
     def place(kx, ky, kc):
         return {name: {'tx': kx, 'ty': ky, 'panel': kc}.get(name, 0) for name in axis_names}
@@ -184,7 +187,8 @@
     def lane_to_idx(spot):
         b = spot // 8
         half = (b + 1) // 2
-        return TILES * lax.rem(spot, 8) + 8 - half + 2 * half * (1 - lax.rem(b, 2))
+        group = jnp.where(b > 2 * CENTRE, b, CENTRE - half + 2 * half * (1 - lax.rem(b, 2)))
+        return TILES * lax.rem(spot, 8) + group
 
     def dot(lhs, rhs):
         return jnp.dot(lhs, rhs, precision=HIGHEST, preferred_element_type=jnp.float32)
@@ -198,7 +202,8 @@
     halo_lane = (lane_s >= 6) | edge_lane
 
     def group_lane(group, number):
-        return 8 * jnp.where(group < 8, 15 - 2 * group, 2 * group - TILES) + number
+        turns = jnp.where(group < CENTRE, 2 * (CENTRE - group) - 1, 2 * (group - CENTRE))
+        return 8 * jnp.where(group > 2 * CENTRE, group, turns) + number
 
     def mirror_lane(group, number):
         return group_lane(lax.rem(19 - group, TILES), jnp.where(group < 4, 11, EDGE) - number)

time: 176 us -> 175 us (level)
  Pallas kernels: 175 us -> 173 us
    pallas_call x1, Pallas kernels: 175 us -> 173 us  [local_run(): pl.pallas_call(functools.partial(kernel, own, steps, axis_names), out_sha...]
where the time goes in v8:
time: 175 us; the launch traced here: 174 us
  Pallas kernels  173 us (99%)
    pallas_call x1, Pallas kernels, local_run(): pl.pallas_call(functools.partial(kernel, own, steps, axis_names), out_sha...  173 us

profile of v8, /device:TPU:0, one launch (start us, length us, event | category | flops | bytes accessed | tf_op | source)
XLA Modules:
  0.0 174.5 jit_solution(3603677305929038630)
XLA Ops:
  0.0 172.9 %advect.1 = f32[3,90,90]{2,1,0:T(8,128)} custom-call(f32[256]{0:T(256)} %ws_in.1, f32[3,90,90]{2,1,0:T(8,128)} %q_in.1, f32[3,90,90]{2,1,0:T(8,128)} %wa_in.1, f32[3,90,90]{2,1,0:T(8,128)} %wb_in.1, f32[128,128]{1,0:T(8,128)} %constant.2.clone.gain_in), custom_call_target="tpu_custom_call" | custom-call | tf_op jit(solution)/shard_map/advect/pallas_call | solution.py:86
  172.9 1.6 copy.7

commit v9 on v8

--- a/solution.py
+++ b/solution.py
@@ -14,7 +14,8 @@
 MESH = pl.DeviceIdType.MESH
 HIGHEST = lax.Precision.HIGHEST
 
-TWIN = tuple(k ^ 1 for k in range(6))
+ARRAYS = range(6)
+TWIN = tuple(k ^ 1 for k in ARRAYS)
 ACROSS = (2, 4, 0, 5, 1, 3)
 PRIMARY = (0, 2, 4)
 STRIPS = ((2, 4), (0, 5), (1, 3))
@@ -105,6 +106,7 @@
                 pltpu.VMEM((4, 3, 8, SIZE), jnp.float32),
             ] + [pltpu.SemaphoreType.DMA(shape) for shape in ((4, 6), (3, 3), (3,)) for _ in range(2)] + [
                 pltpu.SemaphoreType.DMA((5,)),
+                pltpu.SemaphoreType.REGULAR,
             ],
             compiler_params=pltpu.CompilerParams(collective_id=0, has_side_effects=True),
             name="advect",
@@ -119,7 +121,7 @@
 
 def kernel(own, steps, axis_names, ws_in, q_in, wa_in, wb_in, gain_in, out_ref,
            ws_ref, fields, qa_rows, qb_rows, sw, wf, wlast, coef, tiles, result, send, recv, csend, crecv,
-           ssem, rsem, tsend, trecv, osend, orecv, isem):
+           ssem, rsem, tsend, trecv, osend, orecv, isem, second):
     tx, ty, core = lax.axis_index('tx'), lax.axis_index('ty'), lax.axis_index('panel')
     by, bz, bx = tx, ty, lax.rem(core + tx + 1, 2)
     qa, qb = (rows.at[:, pl.ds(0, SIZE)] for rows in (qa_rows, qb_rows))
@@ -127,10 +129,13 @@
     def place(kx, ky, kc):
         return {name: {'tx': kx, 'ty': ky, 'panel': kc}.get(name, 0) for name in axis_names}
 
+    def greet(semaphore):
+        for other in (1, 2, 4, 5, 6):
+            near = [1 - at if other & bit else at for at, bit in ((tx, 1), (ty, 2), (core, 4))]
+            pl.semaphore_signal(semaphore, inc=1, device_id=place(*near), device_id_type=MESH)
+
     barrier = pltpu.get_barrier_semaphore()
-    for other in range(1, 8):
-        near = [1 - at if other & bit else at for at, bit in ((tx, 1), (ty, 2), (core, 4))]
-        pl.semaphore_signal(barrier, inc=1, device_id=place(*near), device_id_type=MESH)
+    greet(barrier)
     loads = [pltpu.make_async_copy(src, dst, isem.at[n]) for n, (src, dst) in enumerate((
         (wa_in, fields.at[1]), (wb_in, fields.at[2]), (q_in, fields.at[0]), (gain_in, coef.at[0]), (ws_in, ws_ref)))]
     for load in loads:
@@ -162,7 +167,8 @@
 
     for load in loads:
         load.wait()
-    pl.semaphore_wait(barrier, 7)
+    pl.semaphore_wait(barrier, 5)
+    greet(second)
     for f in (1, 2, 0):
         for slot in range(3):
             ox, oy, oz, quad = homes[slot]
@@ -367,6 +373,7 @@
                 sw[0, plain] = loc
                 qb[turned] = turn(loc)
         if f == 2:
+            pl.semaphore_wait(second, 5)
             list(sender(qb, 1, 2, sign=-1.0))
             list(sender(sw.at[0], 2, 3, corner_sign=-1.0))
     list(sender(qa, 0, 0))
@@ -377,9 +384,9 @@
 
     wait_all(1, 2)
     wait_all(2, 3)
-    for k in range(6):
+    for k in ARRAYS:
         merge(qb, k, halo_tiles(k, 2), turn(join(halo_tiles(TWIN[k], 3))))
-    for k in range(6):
+    for k in ARRAYS:
         here = qb[k]
         scaled = 0.5 / (6.0 * C_SPEED)
         after = join([here[8:], roll_rows(here[:8], -1)])
@@ -437,7 +444,7 @@
             if sends is not None:
                 next(sends)
         if sends is None and scale is None:
-            for k in range(6):
+            for k in ARRAYS:
                 near = new[ACROSS[k]]
                 dst[k, row(14, 7)] = near[8:9]
                 dst[k, row(15, 7)] = near[:1]

time: 175 us -> 174 us (level)
  no operation moved by 1% of the time
where the time goes in v9:
time: 174 us
  Pallas kernels  173 us (99%)
    pallas_call x1, Pallas kernels, local_run(): pl.pallas_call(functools.partial(kernel, own, steps, axis_names), out_sha...  173 us

profile of v9, /device:TPU:0, one launch (start us, length us, event | category | flops | bytes accessed | tf_op | source)
XLA Modules:
  0.0 174.1 jit_solution(391431482864234498)
XLA Ops:
  0.0 172.6 %advect.1 = f32[3,90,90]{2,1,0:T(8,128)} custom-call(f32[256]{0:T(256)} %ws_in.1, f32[3,90,90]{2,1,0:T(8,128)} %q_in.1, f32[3,90,90]{2,1,0:T(8,128)} %wa_in.1, f32[3,90,90]{2,1,0:T(8,128)} %wb_in.1, f32[128,128]{1,0:T(8,128)} %constant.2.clone.gain_in), custom_call_target="tpu_custom_call" | custom-call | tf_op jit(solution)/shard_map/advect/pallas_call | solution.py:87
  172.6 1.6 copy.7

commit v10 on v9

--- a/solution.py
+++ b/solution.py
@@ -24,11 +24,11 @@
 
 SIZE = 128
 TILES = 16
-PITCH = SIZE + 16
-CENTRE = 5
+PITCH = SIZE + 48
+CENTRE = 7
 EDGE = 10
 BLOCK_STEPS = 10
-GROUPS = ((0, 2), (1, 3), (4, 5))
+FIRST, SECOND, THIRD = GROUPS = ((0, 2), (1, 3), (5, 4))
 
 
 def row_idx(row):
@@ -336,7 +336,7 @@
         wait_all(0, slot)
         halos = {k: halo_tiles(k, slot) for k in (0, 2, 5, 1, 3, 4)}
         lanes = {TWIN[k]: turn(join(halos[k])) for k in (0, 2, 5, 1, 3, 4)}
-        for k in (0, 2, 4, 1, 3, 5):
+        for k in (*SECOND, *FIRST, 4, 5):
             merge(qa, k, halos[k], lanes[k])
 
     def scale_faces(first_step):
@@ -435,10 +435,13 @@
             more = parts_of(src, dst, second, step, group, ghosts, scale, slot)
             part.update(more[0])
             turned.update(more[1])
+            if group is FIRST:
+                for k in group:
+                    dst[k] = part[k]
         new = {}
-        for group in ((1, 3), (0, 2), (4, 5)):
+        for group in (SECOND, FIRST, THIRD):
             for k in group:
-                new[k] = part[k] + turned[TWIN[k]]
+                new[k] = (dst[k] if group is FIRST else part[k]) + turned[TWIN[k]]
             for k in group:
                 dst[k] = new[k]
             if sends is not None:

time: 174 us -> 173 us (level)
  no operation moved by 1% of the time
where the time goes in v10:
time: 173 us
  Pallas kernels  172 us (99%)
    pallas_call x1, Pallas kernels, local_run(): pl.pallas_call(functools.partial(kernel, own, steps, axis_names), out_sha...  172 us

profile of v10, /device:TPU:0, one launch (start us, length us, event | category | flops | bytes accessed | tf_op | source)
XLA Modules:
  0.0 173.3 jit_solution(13036697250284031407)
XLA Ops:
  0.0 171.7 %advect.1 = f32[3,90,90]{2,1,0:T(8,128)} custom-call(f32[256]{0:T(256)} %ws_in.1, f32[3,90,90]{2,1,0:T(8,128)} %q_in.1, f32[3,90,90]{2,1,0:T(8,128)} %wa_in.1, f32[3,90,90]{2,1,0:T(8,128)} %wb_in.1, f32[128,128]{1,0:T(8,128)} %constant.2.clone.gain_in), custom_call_target="tpu_custom_call" | custom-call | tf_op jit(solution)/shard_map/advect/pallas_call | solution.py:87
  171.7 1.6 copy.7
